TPU v7x, 32 devices: a whole 2x2x4 slice. The times are simulated.
32 devices in a mesh: parts: 2 (over x), expert: 16 (over z, y, core).
Axes of the slice: x: 2, y: 2, z: 4, core: 2. Of those that a mesh axis runs over, the one named last changes fastest.
Arguments:
- tokens: bfloat16 [2, 128, 7168], P(None, ('parts', 'expert')), parts along dimension 1, may hold values from -6 to 6
- live_rows: int32 [2, 32], P(None, ('parts', 'expert')), parts along dimension 1, may hold values from 3 to 4
- expert_ids: int32 [1, 2, 128, 8], P(None, None, ('parts', 'expert')), parts along dimension 2, may hold values from 0 to 15, all different within a row; in each aligned block of 4 rows (0 to 3, 4 to 7, ..., all dimensions but the last counted through in order) at most 2 rows name the same one
- gate_weights: float32 [1, 2, 128, 8], P(None, None, ('parts', 'expert')), parts along dimension 2, may hold values from 0.25 to 2.5
- norm_gain: float32 [1, 7168], replicated, may hold values from 0.1 to 1.9
- expert_gate_up: bfloat16 [1, 16, 7168, 2048], P(None, 'expert'), may hold values from -0.0625 to 0.0625
- expert_down: bfloat16 [1, 16, 1024, 7168], P(None, 'expert'), may hold values from -0.1875 to 0.1875
- shared_gate_up: bfloat16 [1, 7168, 2048], P(None, 'expert'), may hold values from -0.0625 to 0.0625
- shared_down: bfloat16 [1, 1024, 7168], P(None, None, 'expert'), may hold values from -0.1875 to 0.1875
Outputs:
- hidden_out: bfloat16 [2, 128, 7168], P(None, ('parts', 'expert')), parts along dimension 1
There are 2 independent parts, one for each index of `parts`. A program takes and returns all parts, laid end to end along the dimension named above; an argument that names none is the same for every part. Nothing has to cross between parts.
Inputs may be any that keep to these rules, and one draw needn't show every extreme that they name: `expert_ids`: the 8 ids of a row differ; within the rows of one device for one layer and step, no expert is named by more than 2 rows, a bound that some block reaches.
All inputs are finite; a program needn't handle non-finite values.
Results may differ from a plain program's by a relative error of at most 0.0068.
Values may be sent and summed in bfloat16 or wider, within the bound.
A program may use at most 128 MiB of HBM per device.

v0:
```python
import functools

import jax
import jax.numpy as jnp
from jax import lax
from jax.experimental import pallas as pl
from jax.experimental.pallas import tpu as pltpu
from jax.sharding import PartitionSpec as P

EXPERTS = 16
EPSILON = 1e-06
LANES = 128
BF16 = jnp.bfloat16
F32 = jnp.float32


def dotted(left, right):
    return jnp.dot(left, right, preferred_element_type=F32)


def dotted_nt(left, right):
    return lax.dot_general(left, right, (((1,), (1,)), ((), ())), preferred_element_type=F32)


def layer_kernel(
    n,
    experts,
    group,
    chunk,
    window,
    tokens_ref,
    live_ref,
    ids_ref,
    gates_ref,
    gain_ref,
    gate_up_hbm,
    down_hbm,
    shared_up_hbm,
    shared_down_hbm,
    update_out,
    acc,
    own_n,
    peer_n,
    x_all,
    gate_up,
    down,
    shared_up,
    shared_down,
    hidden,
    sh_part,
    sh_send,
    sh_peer,
    sh_y,
    sh_yr,
    sh_z,
    sh_zr,
    sh_hidden,
    so_send,
    so_recv,
    so_f,
    so_fr,
    part,
    r_p,
    r_pr,
    r_y,
    r_yr,
    r_z,
    r_zr,
    keep,
    res,
    res_r,
    w_sem,
    n_sem,
    xz_s,
    xy_s,
    xp_s,
    x_r,
    hz_s,
    hy_s,
    hp_s,
    h_r,
    sp_sem,
    sy_sem,
    sz_s,
    sz_r,
    so_s,
    so_r,
    p_s,
    p_r,
    y_s,
    y_r,
    z_s,
    z_r,
    f_sem,
):
    nc = n // 2
    na = nc // 2
    me = lax.axis_index("expert")
    c = lax.rem(me, 2)
    chip = lax.div(me, 2)
    b = lax.rem(chip, 2)
    a = lax.div(chip, 2)
    slot = b * na + a
    oc = 1 - c
    steps, rows_dev, width = tokens_ref.shape
    half = width // 2
    rows = steps * rows_dev
    pair = 2 * rows
    total_rows = nc * pair
    y_rows = na * pair
    units = down.shape[0]
    s_units = sh_part.shape[2]
    fb = shared_down.shape[0]

    def dev(a_at, b_at, c_at):
        return {"expert": (2 * a_at + b_at) * 2 + c_at}

    partner = dev(a, b, oc)
    across = dev(a, 1 - b, c)

    def rcopy(src, dst, send, recv, to):
        return pltpu.make_async_remote_copy(
            src_ref=src,
            dst_ref=dst,
            send_sem=send,
            recv_sem=recv,
            device_id=to,
            device_id_type=pl.DeviceIdType.MESH,
        )

    def a_of(d):
        return lax.rem(a + d, na)

    def a_from(d):
        return lax.rem(a + na - d, na)

    def block(at):
        return pl.ds(pl.multiple_of(at * pair, pair), pair)

    up_rows = width // 8
    loads = []
    offset = lax.rem(me, nc) * fb
    start = pl.multiple_of(lax.div(offset, LANES) * LANES, LANES)
    inner = pl.multiple_of(offset - start, 16)
    loads.append(
        pltpu.make_async_copy(
            shared_up_hbm.at[0], shared_up.at[pl.ds(inner, fb)], w_sem.at[0]
        )
    )
    loads.append(pltpu.make_async_copy(shared_down_hbm.at[0], shared_down, w_sem.at[1]))
    for at in range(8):
        piece = pl.ds(at * up_rows, up_rows)
        loads.append(
            pltpu.make_async_copy(
                gate_up_hbm.at[0, 0, piece], gate_up.at[piece], w_sem.at[2 + at]
            )
        )
    down_rows = units // 4
    for at in range(4):
        piece = pl.ds(at * down_rows, down_rows)
        loads.append(
            pltpu.make_async_copy(down_hbm.at[0, 0, piece], down.at[piece], w_sem.at[10 + at])
        )
    shared_up[...] = jnp.zeros_like(shared_up)

    barrier = pltpu.get_barrier_semaphore()

    def greet(to):
        pl.semaphore_signal(barrier, inc=1, device_id=to, device_id_type=pl.DeviceIdType.MESH)

    greet(partner)
    for d in range(1, nc):
        other = lax.rem(chip + d, nc)
        greet({"expert": other * 2 + c})
    for load in loads:
        load.start()

    lane = lax.broadcasted_iota(jnp.int32, (rows_dev, LANES), 1)
    row_at = lax.broadcasted_iota(jnp.int32, (rows_dev, LANES), 0)
    of_lane = lane & (experts - 1)
    level = lax.div(lane, experts)
    gain = gain_ref[...]
    for step in range(steps):
        h = tokens_ref[step].astype(F32)
        scaling = lax.rsqrt(jnp.mean(h * h, axis=-1, keepdims=True) + EPSILON)
        normed = (h * scaling * gain).astype(BF16).astype(F32)
        ids = ids_ref[0, step]
        gates = gates_ref[0, step]
        dense = jnp.zeros((rows_dev, LANES), F32)
        for k in range(ids.shape[1]):
            dense = dense + jnp.where(ids[:, k : k + 1] == of_lane, gates[:, k : k + 1], 0.0)
        dense = jnp.where(row_at < live_ref[:, step : step + 1], dense, 0.0)
        high = dense.astype(BF16).astype(F32)
        rest = dense - high
        mid = rest.astype(BF16).astype(F32)
        low = rest - mid
        coded = jnp.where(
            level == 0, high, jnp.where(level == 1, mid, jnp.where(level == 2, low, 0.0))
        )
        at = slice(step * rows_dev, (step + 1) * rows_dev)
        for side in range(2):
            own_n[side, at, :half] = normed[:, side * half : (side + 1) * half]
            own_n[side, at, half:] = coded

    pl.semaphore_wait(barrier, nc)

    swap = rcopy(own_n.at[oc], peer_n, n_sem.at[0], n_sem.at[1], partner)
    swap.start()
    swap.wait()
    mine = own_n[c]
    theirs = peer_n[...]
    first = jnp.where(c == 0, mine, theirs)
    second = jnp.where(c == 0, theirs, mine)
    x_all[c, block(slot)] = jnp.concatenate([first, second], axis=0).astype(BF16)

    def gather(buf, zs, ys, ps, rs):
        sent = []

        def push(at, send, to):
            copy = rcopy(buf.at[c, block(at)], buf.at[c, block(at)], send, rs.at[c, at], to)
            copy.start()
            sent.append(copy)

        def arrived(side, at):
            view = buf.at[side, block(at)]
            rcopy(view, view, ps.at[0], rs.at[side, at], partner).wait_recv()

        def begin():
            for d in range(1, na):
                push(slot, zs.at[d], dev(a_of(d), b, c))
            push(slot, ys.at[0], across)
            push(slot, ps.at[0], partner)

        def forward():
            for d in range(1, na):
                at = b * na + a_from(d)
                arrived(c, at)
                push(at, ys.at[d], across)
                push(at, ps.at[d], partner)

        def finish():
            for d in range(na):
                at = (1 - b) * na + a_from(d)
                arrived(c, at)
                push(at, ps.at[na + d], partner)
            for at in range(nc):
                arrived(oc, at)

        return begin, forward, finish, sent

    begin, forward, finish, sent = gather(x_all, xz_s, xy_s, xp_s, x_r)
    begin()
    forward()
    finish()
    pending = list(sent)

    expert = lax.div(me, group)
    codes = x_all[0, :, half:].astype(F32)
    wide = lax.broadcasted_iota(jnp.int32, (total_rows, LANES), 1) & (experts - 1)
    weight = jnp.sum(jnp.where(wide == expert, codes, 0.0), axis=1, keepdims=True)

    s_half = s_units // 2

    def shared_project():
        loads[0].wait()
        features = x_all[lax.div(me, nc), :, pl.ds(start, window)]
        for side in range(2):
            for kind in range(2):
                cols = slice(kind * s_units + side * s_half, kind * s_units + (side + 1) * s_half)
                sh_part[side, :, kind * s_half : (kind + 1) * s_half] = dotted(
                    features, shared_up[:, cols]
                )
        sh_send[...] = sh_part[oc].astype(BF16)
        copy = rcopy(sh_send, sh_peer, sp_sem.at[0], sp_sem.at[1], partner)
        copy.start()
        return copy

    y_own = pl.ds(pl.multiple_of(b * y_rows, y_rows), y_rows)
    y_other = pl.ds(pl.multiple_of((1 - b) * y_rows, y_rows), y_rows)

    def shared_across(copy):
        copy.wait()
        sh_y[...] = (sh_part[c, y_other] + sh_peer[y_other].astype(F32)).astype(BF16)
        out = rcopy(sh_y, sh_yr, sy_sem.at[0], sy_sem.at[1], across)
        out.start()
        return out

    def shared_along(copy):
        copy.wait()
        summed = sh_part[c, y_own] + sh_peer[y_own].astype(F32) + sh_yr[...].astype(F32)
        sh_part[0, :y_rows] = summed
        sh_z[...] = summed.astype(BF16).reshape(na, pair, s_units)
        copies = []
        for d in range(1, na):
            copy = rcopy(
                sh_z.at[a_of(d)],
                sh_zr.at[d],
                sz_s.at[d],
                sz_r.at[d],
                dev(a_of(d), b, c),
            )
            copy.start()
            copies.append(copy)
        return copies

    h_begin, h_forward, h_finish, h_sent = gather(sh_hidden, hz_s, hy_s, hp_s, h_r)

    def shared_active(copies):
        total = sh_part[0, block(a)]
        for d in range(1, na):
            copies[d - 1].wait()
            total = total + sh_zr[d].astype(F32)
        sh_hidden[c, block(slot)] = (
            jax.nn.silu(total[:, :s_half]) * total[:, s_half:]
        ).astype(BF16)
        h_begin()

    def shared_last():
        h_finish()
        pending.extend(h_sent)
        loads[1].wait()
        cols = dotted_nt(sh_hidden[0], shared_down[:, :s_half]) + dotted_nt(
            sh_hidden[1], shared_down[:, s_half:]
        )
        so_send[...] = cols.astype(BF16).reshape(nc, pair, fb)
        copies = []
        for d in range(1, nc):
            other = lax.rem(chip + d, nc)
            to_slot = lax.rem(other, 2) * na + lax.div(other, 2)
            copy = rcopy(
                so_send.at[to_slot],
                so_recv.at[chip],
                so_s.at[d],
                so_r.at[chip],
                {"expert": other * 2 + c},
            )
            copy.start()
            copies.append(copy)
        return copies

    def shared_collect(copies):
        for d in range(1, nc):
            other = lax.rem(chip + nc - d, nc)
            view = so_recv.at[other]
            rcopy(view, view, so_s.at[0], so_r.at[other], partner).wait_recv()
        so_recv[chip] = so_send[slot]
        for at in range(nc):
            value = so_recv[at].astype(F32)
            so_f[0, at] = value[:rows]
            so_f[1, at] = value[rows:]
        copy = rcopy(so_f.at[oc], so_fr, f_sem.at[2], f_sem.at[3], partner)
        copy.start()
        for copy_at in copies:
            copy_at.wait_send()
        return copy

    def gate_up_tile(at, tile):
        def product(first_col):
            cols = slice(first_col, first_col + tile)
            return dotted(x_all[0, :, :half], gate_up[:half, cols]) + dotted(
                x_all[1, :, :half], gate_up[half:, cols]
            )

        gate = product(at * tile)
        up = product(units + at * tile)
        hidden[:, at * tile : (at + 1) * tile] = (jax.nn.silu(gate) * up).astype(BF16)

    state = [shared_project()]
    for load in loads[2:10]:
        load.wait()
    tile = min(256, units)
    for at in range(units // tile):
        gate_up_tile(at, tile)
        if at == 0:
            state.append(shared_across(state[-1]))
    for load in loads[10:]:
        load.wait()

    chunks = half // chunk

    def product(side, j):
        cols = pl.ds(pl.multiple_of(side * half + j * chunk, LANES), chunk)
        return dotted(hidden[...], down[:, cols]) * weight

    to_partner = []

    def send_partner(j):
        r_p[j] = product(oc, j).astype(BF16)
        copy = rcopy(r_p.at[j], r_pr.at[j], p_s.at[j], p_r.at[j], partner)
        copy.start()
        to_partner.append(copy)

    to_across = []
    to_along = []

    def send_across(j):
        part[...] = product(c, j)
        to_partner[j].wait()
        r_y[j] = (part[y_other] + r_pr[j, y_other].astype(F32)).astype(BF16)
        copy = rcopy(r_y.at[j], r_yr.at[j], y_s.at[j], y_r.at[j], across)
        copy.start()
        to_across.append(copy)
        keep[j] = part[y_own] + r_pr[j, y_own].astype(F32)

    def send_along(j):
        to_across[j].wait()
        summed = keep[j] + r_yr[j].astype(F32)
        r_z[j] = summed.astype(BF16).reshape(na, pair, chunk)
        copies = []
        for d in range(1, na):
            copy = rcopy(
                r_z.at[j, a_of(d)],
                r_zr.at[j, d],
                z_s.at[j, d],
                z_r.at[j, d],
                dev(a_of(d), b, c),
            )
            copy.start()
            copies.append(copy)
        to_along.append(copies)
        keep[j] = summed

    def collect(j):
        total = keep[j, block(a)]
        for d in range(1, na):
            to_along[j][d - 1].wait()
            total = total + r_zr[j, d].astype(F32)
        cols = slice(j * chunk, (j + 1) * chunk)
        res[0, :, cols] = total[:rows]
        res[1, :, cols] = total[rows:]

    stages = {
        0: lambda: state.append(shared_along(state[-1])),
        2: lambda: shared_active(state[-1]),
        4: h_forward,
        5: lambda: state.append(shared_last()),
    }
    for j in range(min(2, chunks)):
        send_partner(j)
    for j in range(max(chunks, 6)):
        if j + 2 < chunks:
            send_partner(j + 2)
        if j < chunks:
            send_across(j)
        if 2 <= j and j - 2 < chunks:
            send_along(j - 2)
        if j in stages:
            stages[j]()
    for j in range(max(chunks, 6) - 2, chunks):
        send_along(j)
    so_copies = state[-1]
    shared_swap = shared_collect(so_copies)
    for j in range(chunks):
        collect(j)
    last = rcopy(res.at[oc], res_r, f_sem.at[0], f_sem.at[1], partner)
    last.start()
    own_cols = pl.ds(pl.multiple_of(c * half, LANES), half)
    other_cols = pl.ds(pl.multiple_of(oc * half, LANES), half)
    acc[:, own_cols] = res[c]
    shared_swap.wait()
    last.wait()
    acc[:, other_cols] = res_r[...]
    for at in range(nc):
        slot_chip = so_f[c, at]
        peer_chip = so_fr[at]
        for side in range(2):
            cols = slice((2 * at + side) * fb, (2 * at + side + 1) * fb)
            acc[:, cols] = acc[:, cols] + jnp.where(c == side, slot_chip, peer_chip)
    for step in range(steps):
        update_out[step] = acc[step * rows_dev : (step + 1) * rows_dev]
    for copy in pending:
        copy.wait_send()


def per_device(
    tokens,
    live_rows,
    expert_ids,
    gate_weights,
    norm_gain,
    expert_gate_up,
    expert_down,
    shared_gate_up,
    shared_down,
):
    step_count, row_count, model_width = tokens.shape
    n = lax.axis_size("expert")
    group = n // EXPERTS
    units = expert_down.shape[2]
    fb, s_wide = shared_gate_up.shape[1:]
    s_units = s_wide // 2
    nc = n // 2
    na = nc // 2
    half = model_width // 2
    rows = step_count * row_count
    pair = 2 * rows
    total = nc * pair
    y_rows = na * pair
    wide = half + LANES
    chunk = next(size for size in (512, 256, 128) if half % size == 0)
    chunks = half // chunk
    span = next(size for size in (128, 64, 32, 16) if fb % size == 0)
    window = -(-(fb + LANES - span) // LANES) * LANES
    dma = pltpu.SemaphoreType.DMA
    vmem = pltpu.VMEM
    whole = pl.BlockSpec(memory_space=pltpu.VMEM)
    anywhere = pl.BlockSpec(memory_space=pl.ANY)
    update = pl.pallas_call(
        functools.partial(layer_kernel, n, EXPERTS, group, chunk, window),
        out_shape=jax.ShapeDtypeStruct(tokens.shape, F32),
        in_specs=[whole] * 5 + [anywhere] * 4,
        out_specs=whole,
        scratch_shapes=[
            vmem((rows, model_width), F32),
            vmem((2, rows, wide), F32),
            vmem((rows, wide), F32),
            vmem((2, total, wide), BF16),
            vmem((model_width, 2 * units), BF16),
            vmem((units, model_width), BF16),
            vmem((window, s_wide), BF16),
            vmem((fb, s_units), BF16),
            vmem((total, units), BF16),
            vmem((2, total, s_units), F32),
            vmem((total, s_units), BF16),
            vmem((total, s_units), BF16),
            vmem((y_rows, s_units), BF16),
            vmem((y_rows, s_units), BF16),
            vmem((na, pair, s_units), BF16),
            vmem((na, pair, s_units), BF16),
            vmem((2, total, s_units // 2), BF16),
            vmem((nc, pair, fb), BF16),
            vmem((nc, pair, fb), BF16),
            vmem((2, nc, rows, fb), F32),
            vmem((nc, rows, fb), F32),
            vmem((total, chunk), F32),
            vmem((chunks, total, chunk), BF16),
            vmem((chunks, total, chunk), BF16),
            vmem((chunks, y_rows, chunk), BF16),
            vmem((chunks, y_rows, chunk), BF16),
            vmem((chunks, na, pair, chunk), BF16),
            vmem((chunks, na, pair, chunk), BF16),
            vmem((chunks, y_rows, chunk), F32),
            vmem((2, rows, half), F32),
            vmem((rows, half), F32),
            dma((14,)),
            dma((2,)),
            dma((na,)),
            dma((na,)),
            dma((nc,)),
            dma((2, nc)),
            dma((na,)),
            dma((na,)),
            dma((nc,)),
            dma((2, nc)),
            dma((2,)),
            dma((2,)),
            dma((na,)),
            dma((na,)),
            dma((nc,)),
            dma((nc,)),
            dma((chunks,)),
            dma((chunks,)),
            dma((chunks,)),
            dma((chunks,)),
            dma((chunks, na)),
            dma((chunks, na)),
            dma((4,)),
        ],
        compiler_params=pltpu.CompilerParams(
            collective_id=0, has_side_effects=True, vmem_limit_bytes=67_043_328
        ),
    )(
        tokens,
        live_rows.T,
        expert_ids,
        gate_weights,
        norm_gain,
        expert_gate_up,
        expert_down,
        shared_gate_up,
        jnp.swapaxes(shared_down, 1, 2),
    )
    live = jnp.arange(row_count, dtype=jnp.int32)[None, :] < live_rows
    update = jnp.where(live[:, :, None], update, 0.0)
    return (tokens.astype(F32) + update).astype(BF16)


def solution(mesh):
    placed = (
        P(None, ("parts", "expert"), None),
        P(None, ("parts", "expert")),
        P(None, None, ("parts", "expert"), None),
        P(None, None, ("parts", "expert"), None),
        P(),
        P(None, "expert", None, None),
        P(None, "expert", None, None),
        P(None, "expert", None),
        P(None, None, "expert"),
    )
    return jax.shard_map(
        per_device,
        mesh=mesh,
        in_specs=placed,
        out_specs=P(None, ("parts", "expert"), None),
        check_vma=False,
    )
```

profile of v0, /device:TPU:0, one launch (start us, length us, event | category | flops | bytes accessed | tf_op | source)
XLA Modules:
  0.0 62.9 jit_solution(16477742760913149487)
XLA Ops:
  0.0 1.2 %iota_compare_fusion = pred[2,4]{1,0:T(4,128)(4,1)} fusion(s32[2]{0:T(128)} %bitcast.4), kind=kLoop, calls=%fused_computation.1 | loop fusion | flops 8 | bytes 16 | tf_op jit(solution)/shard_map/lt | solution.py:583
  1.2 59.9 %shard_map.94 = f32[2,4,7168]{2,1,0:T(4,128)} custom-call(bf16[2,4,7168]{2,1,0:T(4,128)(2,1)} %tokens_ref.1, s32[1,2]{1,0:T(1,128)} %bitcast.5, s32[1,2,4,8]{3,2,1,0:T(4,128)} %ids_ref.1, f32[1,2,4,8]{3,2,1,0:T(4,128)} %gates_ref.1, f32[1,7168]{1,0:T(1,128)} %gain_ref.1, bf16[1,1,7168,2048]{3,2,1,0:T(8,128)(2,1)} %gate_up_hbm.1, ...), custom_call_target="tpu_custom_call" | custom-call | tf_op jit(solution)/shard_map/pallas_call | solution.py:508
  61.1 1.8 %add_convert_fusion = bf16[2,4,7168]{2,1,0:T(4,128)(2,1)} fusion(f32[2,4,7168]{2,1,0:T(4,128)} %shard_map.94, bf16[2,4,7168]{2,1,0:T(4,128)(2,1)} %tokens_ref.1, pred[2,4]{1,0:T(4,128)(4,1)} %iota_compare_fusion), kind=kLoop, calls=%fused_computation | loop fusion | flops 229376 | bytes 458760 | tf_op jit(solution)/shard_map/convert_element_type | solution.py:585
where the time goes:
time: 63 us; the launch traced here: 62.9 us
  Pallas kernels  59.9 us (95%)
  other arithmetic  3.01 us (5%)
    pallas_call x1, Pallas kernels, per_device(): pl.pallas_call(functools.partial(layer_kernel, n, EXPERTS, group, chunk,...  59.9 us
    convert_element_type x1, other arithmetic, per_device(): return (tokens.astype(F32) + update).astype(BF16)  1.77 us

commit v1 on v0

--- a/solution.py
+++ b/solution.py
@@ -28,6 +28,7 @@
     group,
     chunk,
     window,
+    x_chunk,
     tokens_ref,
     live_ref,
     ids_ref,
@@ -37,15 +38,17 @@
     down_hbm,
     shared_up_hbm,
     shared_down_hbm,
-    update_out,
+    out_ref,
     acc,
     own_n,
     peer_n,
     x_all,
+    x_win,
     gate_up,
     down,
     shared_up,
     shared_down,
+    up_acc,
     hidden,
     sh_part,
     sh_send,
@@ -59,7 +62,6 @@
     so_recv,
     so_f,
     so_fr,
-    part,
     r_p,
     r_pr,
     r_y,
@@ -71,6 +73,8 @@
     res_r,
     w_sem,
     n_sem,
+    win_s,
+    win_r,
     xz_s,
     xy_s,
     xp_s,
@@ -92,6 +96,7 @@
     z_s,
     z_r,
     f_sem,
+    l_sem,
 ):
     nc = n // 2
     na = nc // 2
@@ -111,12 +116,16 @@
     units = down.shape[0]
     s_units = sh_part.shape[2]
     fb = shared_down.shape[0]
+    x_count = half // x_chunk
+    chunks = half // chunk
 
     def dev(a_at, b_at, c_at):
         return {"expert": (2 * a_at + b_at) * 2 + c_at}
 
     partner = dev(a, b, oc)
     across = dev(a, 1 - b, c)
+    below = dev(a - 1, b, c)
+    above = dev(a + 1, b, c)
 
     def rcopy(src, dst, send, recv, to):
         return pltpu.make_async_remote_copy(
@@ -137,41 +146,48 @@
     def block(at):
         return pl.ds(pl.multiple_of(at * pair, pair), pair)
 
-    up_rows = width // 8
     loads = []
     offset = lax.rem(me, nc) * fb
-    start = pl.multiple_of(lax.div(offset, LANES) * LANES, LANES)
+    start = lax.div(offset, LANES) * LANES
     inner = pl.multiple_of(offset - start, 16)
     loads.append(
         pltpu.make_async_copy(
             shared_up_hbm.at[0], shared_up.at[pl.ds(inner, fb)], w_sem.at[0]
         )
     )
-    loads.append(pltpu.make_async_copy(shared_down_hbm.at[0], shared_down, w_sem.at[1]))
-    for at in range(8):
-        piece = pl.ds(at * up_rows, up_rows)
-        loads.append(
-            pltpu.make_async_copy(
-                gate_up_hbm.at[0, 0, piece], gate_up.at[piece], w_sem.at[2 + at]
+    for at in range(x_count):
+        for side in range(2):
+            piece = pl.ds(side * half + at * x_chunk, x_chunk)
+            loads.append(
+                pltpu.make_async_copy(
+                    gate_up_hbm.at[0, 0, piece],
+                    gate_up.at[piece],
+                    w_sem.at[1 + 2 * at + side],
+                )
             )
-        )
+    down_first = len(loads)
     down_rows = units // 4
     for at in range(4):
         piece = pl.ds(at * down_rows, down_rows)
         loads.append(
-            pltpu.make_async_copy(down_hbm.at[0, 0, piece], down.at[piece], w_sem.at[10 + at])
+            pltpu.make_async_copy(
+                down_hbm.at[0, 0, piece], down.at[piece], w_sem.at[down_first + at]
+            )
         )
+    shared_down_at = len(loads)
+    loads.append(
+        pltpu.make_async_copy(shared_down_hbm.at[0], shared_down, w_sem.at[shared_down_at])
+    )
     shared_up[...] = jnp.zeros_like(shared_up)
 
     barrier = pltpu.get_barrier_semaphore()
-
-    def greet(to):
-        pl.semaphore_signal(barrier, inc=1, device_id=to, device_id_type=pl.DeviceIdType.MESH)
-
-    greet(partner)
-    for d in range(1, nc):
-        other = lax.rem(chip + d, nc)
-        greet({"expert": other * 2 + c})
+    for d in range(1, n):
+        pl.semaphore_signal(
+            barrier,
+            inc=1,
+            device_id={"expert": lax.rem(me + d, n)},
+            device_id_type=pl.DeviceIdType.MESH,
+        )
     for load in loads:
         load.start()
 
@@ -202,7 +218,7 @@
             own_n[side, at, :half] = normed[:, side * half : (side + 1) * half]
             own_n[side, at, half:] = coded
 
-    pl.semaphore_wait(barrier, nc)
+    pl.semaphore_wait(barrier, n - 1)
 
     swap = rcopy(own_n.at[oc], peer_n, n_sem.at[0], n_sem.at[1], partner)
     swap.start()
@@ -213,6 +229,96 @@
     second = jnp.where(c == 0, theirs, mine)
     x_all[c, block(slot)] = jnp.concatenate([first, second], axis=0).astype(BF16)
 
+    def window_copy(i):
+        lo = i * fb // LANES * LANES
+        source = x_all.at[c, block(slot), pl.ds(lo, window)]
+        return source, x_win.at[slot], win_r.at[slot], c * nc + i
+
+    for i in range(nc):
+        source, target, recv, to = window_copy(i)
+
+        @pl.when(to != me)
+        def _():
+            rcopy(source, target, win_s.at[i], recv, {"expert": to}).start()
+
+        @pl.when(to == me)
+        def _():
+            pltpu.make_async_copy(source, target, recv).start()
+
+    def x_view(side, at, k):
+        wide = x_chunk + (LANES if k == x_count - 1 else 0)
+        return x_all.at[side, block(at), pl.ds(k * x_chunk, wide)]
+
+    def x_push(at, k, send, to):
+        view = x_view(c, at, k)
+        rcopy(view, view, send, x_r.at[c, at, k], to).start()
+
+    def x_arrived(side, at, k):
+        view = x_view(side, at, k)
+        rcopy(view, view, xp_s.at[0], x_r.at[side, at, k], partner).wait_recv()
+
+    def x_pass(source, k, down_line, up_line):
+        at = b * na + source
+
+        @pl.when(down_line & (a > 0))
+        def _():
+            x_push(at, k, xz_s.at[0, source], below)
+
+        @pl.when(up_line & (a < na - 1))
+        def _():
+            x_push(at, k, xz_s.at[1, source], above)
+
+        x_push(at, k, xy_s.at[source], across)
+        x_push(at, k, xp_s.at[at], partner)
+
+    def at_distance(d, body):
+        if d == 0:
+            body(a, True, True)
+            return
+
+        @pl.when(a + d < na)
+        def _():
+            body(a + d, True, False)
+
+        @pl.when(a - d >= 0)
+        def _():
+            body(a - d, False, True)
+
+    def x_along(d):
+        for k in range(x_count):
+
+            def one(source, down_line, up_line):
+                if d:
+                    x_arrived(c, b * na + source, k)
+                x_pass(source, k, down_line, up_line)
+
+            at_distance(d, one)
+
+    def x_crossed(d, k):
+        def one(source, down_line, up_line):
+            at = (1 - b) * na + source
+            x_arrived(c, at, k)
+            x_push(at, k, xp_s.at[at], partner)
+
+        at_distance(d, one)
+
+    def x_sent(source, down_line, up_line):
+        at = b * na + source
+        view = x_all.at[c, block(at)]
+        other = (1 - b) * na + source
+
+        @pl.when(down_line & (a > 0))
+        def _():
+            rcopy(view, view, xz_s.at[0, source], x_r.at[c, 0, 0], partner).wait_send()
+
+        @pl.when(up_line & (a < na - 1))
+        def _():
+            rcopy(view, view, xz_s.at[1, source], x_r.at[c, 0, 0], partner).wait_send()
+
+        rcopy(view, view, xy_s.at[source], x_r.at[c, 0, 0], partner).wait_send()
+        rcopy(view, view, xp_s.at[at], x_r.at[c, 0, 0], partner).wait_send()
+        rcopy(view, view, xp_s.at[other], x_r.at[c, 0, 0], partner).wait_send()
+
     def gather(buf, zs, ys, ps, rs):
         sent = []
 
@@ -248,22 +354,14 @@
 
         return begin, forward, finish, sent
 
-    begin, forward, finish, sent = gather(x_all, xz_s, xy_s, xp_s, x_r)
-    begin()
-    forward()
-    finish()
-    pending = list(sent)
-
-    expert = lax.div(me, group)
-    codes = x_all[0, :, half:].astype(F32)
-    wide = lax.broadcasted_iota(jnp.int32, (total_rows, LANES), 1) & (experts - 1)
-    weight = jnp.sum(jnp.where(wide == expert, codes, 0.0), axis=1, keepdims=True)
-
     s_half = s_units // 2
 
     def shared_project():
         loads[0].wait()
-        features = x_all[lax.div(me, nc), :, pl.ds(start, window)]
+        for at in range(nc):
+            view = x_win.at[at]
+            rcopy(view, view, win_s.at[0], win_r.at[at], partner).wait_recv()
+        features = x_win[...].reshape(total_rows, window)
         for side in range(2):
             for kind in range(2):
                 cols = slice(kind * s_units + side * s_half, kind * s_units + (side + 1) * s_half)
@@ -317,8 +415,7 @@
 
     def shared_last():
         h_finish()
-        pending.extend(h_sent)
-        loads[1].wait()
+        loads[shared_down_at].wait()
         cols = dotted_nt(sh_hidden[0], shared_down[:, :s_half]) + dotted_nt(
             sh_hidden[1], shared_down[:, s_half:]
         )
@@ -348,128 +445,199 @@
             value = so_recv[at].astype(F32)
             so_f[0, at] = value[:rows]
             so_f[1, at] = value[rows:]
-        copy = rcopy(so_f.at[oc], so_fr, f_sem.at[2], f_sem.at[3], partner)
+        copy = rcopy(so_f.at[oc], so_fr, f_sem.at[0], f_sem.at[1], partner)
         copy.start()
         for copy_at in copies:
             copy_at.wait_send()
         return copy
 
-    def gate_up_tile(at, tile):
-        def product(first_col):
-            cols = slice(first_col, first_col + tile)
-            return dotted(x_all[0, :, :half], gate_up[:half, cols]) + dotted(
-                x_all[1, :, :half], gate_up[half:, cols]
-            )
-
-        gate = product(at * tile)
-        up = product(units + at * tile)
-        hidden[:, at * tile : (at + 1) * tile] = (jax.nn.silu(gate) * up).astype(BF16)
-
-    state = [shared_project()]
-    for load in loads[2:10]:
+    def up_term(k, cols):
+        at = k * x_chunk
+        return dotted(x_all[0, :, at : at + x_chunk], gate_up[at : at + x_chunk, cols]) + dotted(
+            x_all[1, :, at : at + x_chunk], gate_up[half + at : half + at + x_chunk, cols]
+        )
+
+    tile = min(256, units)
+
+    def up_part(k):
+        for at in range(nc):
+            x_arrived(oc, at, k)
+        for side in range(2):
+            loads[1 + 2 * k + side].wait()
+        if k < x_count - 1:
+            for at in range(2 * units // tile):
+                cols = slice(at * tile, (at + 1) * tile)
+                if k == 0:
+                    up_acc[:, cols] = up_term(k, cols)
+                else:
+                    up_acc[:, cols] += up_term(k, cols)
+            return
+        for at in range(units // tile):
+            gate_cols = slice(at * tile, (at + 1) * tile)
+            up_cols = slice(units + at * tile, units + (at + 1) * tile)
+            gate = up_term(k, gate_cols)
+            up = up_term(k, up_cols)
+            if k:
+                gate = gate + up_acc[:, gate_cols]
+                up = up + up_acc[:, up_cols]
+            hidden[:, gate_cols] = (jax.nn.silu(gate) * up).astype(BF16)
+
+    state = []
+    x_along(0)
+    for d in range(1, na):
+        x_along(d)
+        for k in range(x_count):
+            x_crossed(d - 1, k)
+        if d == 1:
+            state.append(shared_project())
+        if d == min(2, na - 1):
+            state.append(shared_across(state[-1]))
+    lag = min(2, x_count - 1)
+    for k in range(x_count + lag):
+        if k < x_count:
+            x_crossed(na - 1, k)
+        if k >= lag:
+            up_part(k - lag)
+            if k - lag == x_count // 2:
+                state.append(shared_along(state[-1]))
+
+    expert = lax.div(me, group)
+    codes = x_all[0, :, half:].astype(F32)
+    wide = lax.broadcasted_iota(jnp.int32, (total_rows, LANES), 1) & (experts - 1)
+    weight = jnp.sum(jnp.where(wide == expert, codes, 0.0), axis=1, keepdims=True)
+
+    for load in loads[down_first:shared_down_at]:
         load.wait()
-    tile = min(256, units)
-    for at in range(units // tile):
-        gate_up_tile(at, tile)
-        if at == 0:
-            state.append(shared_across(state[-1]))
-    for load in loads[10:]:
-        load.wait()
-
-    chunks = half // chunk
 
     def product(side, j):
         cols = pl.ds(pl.multiple_of(side * half + j * chunk, LANES), chunk)
         return dotted(hidden[...], down[:, cols]) * weight
 
-    to_partner = []
-
     def send_partner(j):
         r_p[j] = product(oc, j).astype(BF16)
-        copy = rcopy(r_p.at[j], r_pr.at[j], p_s.at[j], p_r.at[j], partner)
-        copy.start()
-        to_partner.append(copy)
-
-    to_across = []
-    to_along = []
-
-    def send_across(j):
-        part[...] = product(c, j)
-        to_partner[j].wait()
-        r_y[j] = (part[y_other] + r_pr[j, y_other].astype(F32)).astype(BF16)
-        copy = rcopy(r_y.at[j], r_yr.at[j], y_s.at[j], y_r.at[j], across)
-        copy.start()
-        to_across.append(copy)
-        keep[j] = part[y_own] + r_pr[j, y_own].astype(F32)
-
-    def send_along(j):
-        to_across[j].wait()
-        summed = keep[j] + r_yr[j].astype(F32)
-        r_z[j] = summed.astype(BF16).reshape(na, pair, chunk)
-        copies = []
-        for d in range(1, na):
-            copy = rcopy(
-                r_z.at[j, a_of(d)],
-                r_zr.at[j, d],
-                z_s.at[j, d],
-                z_r.at[j, d],
-                dev(a_of(d), b, c),
-            )
-            copy.start()
-            copies.append(copy)
-        to_along.append(copies)
-        keep[j] = summed
+        rcopy(r_p.at[j], r_pr.at[j], p_s.at[0], p_r.at[j], partner).start()
+
+    far = jnp.where(2 * a >= na, 0, na - 1)
+
+    def send_across(at, j):
+        rcopy(r_y.at[at, j], r_yr.at[at, j], y_s.at[at], y_r.at[at, j], across).start()
+
+    def own_part(j):
+        mine = product(c, j)
+        rcopy(r_p.at[j], r_pr.at[j], p_s.at[0], p_r.at[j], partner).wait_recv()
+        up_acc[:, :chunk] = mine
+        other = (up_acc[y_other, :chunk] + r_pr[j, y_other].astype(F32)).astype(BF16)
+        for at in range(na):
+            r_y[at, j] = other[at * pair : (at + 1) * pair]
+        send_across(far, j)
+        here = up_acc[y_own, :chunk] + r_pr[j, y_own].astype(F32)
+        for at in range(na):
+            keep[at, j] = here[at * pair : (at + 1) * pair]
+
+    def y_arrived(at, j):
+        rcopy(r_y.at[at, j], r_yr.at[at, j], y_s.at[at], y_r.at[at, j], across).wait_recv()
+
+    def z_arrived(way, at, j):
+        view = r_zr.at[way, at, j]
+        rcopy(view, view, z_s.at[at], z_r.at[way, at, j], across).wait_recv()
+
+    def z_pass(d, j):
+        def one(at, up_line, down_line):
+            way, inside, to = (1, a > 0, above) if up_line else (0, a < na - 1, below)
+            y_arrived(at, j)
+            summed = keep[at, j] + r_yr[at, j].astype(F32)
+
+            @pl.when(inside)
+            def _():
+                z_arrived(way, at, j)
+                r_z[at, j] = (summed + r_zr[way, at, j].astype(F32)).astype(BF16)
+
+            @pl.when(jnp.logical_not(inside))
+            def _():
+                r_z[at, j] = summed.astype(BF16)
+
+            rcopy(r_z.at[at, j], r_zr.at[way, at, j], z_s.at[at], z_r.at[way, at, j], to).start()
+
+        at_distance(d, one)
 
     def collect(j):
-        total = keep[j, block(a)]
-        for d in range(1, na):
-            to_along[j][d - 1].wait()
-            total = total + r_zr[j, d].astype(F32)
-        cols = slice(j * chunk, (j + 1) * chunk)
-        res[0, :, cols] = total[:rows]
-        res[1, :, cols] = total[rows:]
-
-    stages = {
-        0: lambda: state.append(shared_along(state[-1])),
-        2: lambda: shared_active(state[-1]),
-        4: h_forward,
-        5: lambda: state.append(shared_last()),
-    }
-    for j in range(min(2, chunks)):
+        y_arrived(a, j)
+        keep[a, j] = keep[a, j] + r_yr[a, j].astype(F32)
+        for way, inside in ((1, a > 0), (0, a < na - 1)):
+
+            @pl.when(inside)
+            def _():
+                z_arrived(way, a, j)
+                keep[a, j] = keep[a, j] + r_zr[way, a, j].astype(F32)
+
+        total = keep[a, j]
+        res[0, j] = total[:rows]
+        res[1, j] = total[rows:]
+        rcopy(res.at[oc, j], res_r.at[j], l_sem.at[0, j], l_sem.at[1, j], partner).start()
+
+    lead = min(2, chunks)
+    for j in range(lead):
         send_partner(j)
-    for j in range(max(chunks, 6)):
-        if j + 2 < chunks:
-            send_partner(j + 2)
-        if j < chunks:
-            send_across(j)
-        if 2 <= j and j - 2 < chunks:
-            send_along(j - 2)
-        if j in stages:
-            stages[j]()
-    for j in range(max(chunks, 6) - 2, chunks):
-        send_along(j)
-    so_copies = state[-1]
-    shared_swap = shared_collect(so_copies)
+    for j in range(chunks):
+        if j + lead < chunks:
+            send_partner(j + lead)
+        own_part(j)
+    for d in range(na - 1, -1, -1):
+
+        def rest(at, up_line, down_line):
+            @pl.when(at != far)
+            def _():
+                for j in range(chunks):
+                    send_across(at, j)
+
+        at_distance(d, rest)
+    shared_active(state[-1])
+    for d in range(na - 1, 0, -1):
+        for j in range(chunks):
+            z_pass(d, j)
+        if d == na - 1:
+            h_forward()
+        if d == max(1, na - 2):
+            state.append(shared_last())
+    shared_swap = shared_collect(state[-1])
     for j in range(chunks):
         collect(j)
-    last = rcopy(res.at[oc], res_r, f_sem.at[0], f_sem.at[1], partner)
-    last.start()
-    own_cols = pl.ds(pl.multiple_of(c * half, LANES), half)
-    other_cols = pl.ds(pl.multiple_of(oc * half, LANES), half)
-    acc[:, own_cols] = res[c]
+    for j in range(chunks):
+        rcopy(res.at[oc, j], res_r.at[j], l_sem.at[0, j], l_sem.at[1, j], partner).wait()
+        own_cols = pl.ds(pl.multiple_of(c * half + j * chunk, LANES), chunk)
+        other_cols = pl.ds(pl.multiple_of(oc * half + j * chunk, LANES), chunk)
+        acc[:, own_cols] = res[c, j]
+        acc[:, other_cols] = res_r[j]
     shared_swap.wait()
-    last.wait()
-    acc[:, other_cols] = res_r[...]
     for at in range(nc):
         slot_chip = so_f[c, at]
         peer_chip = so_fr[at]
         for side in range(2):
             cols = slice((2 * at + side) * fb, (2 * at + side + 1) * fb)
             acc[:, cols] = acc[:, cols] + jnp.where(c == side, slot_chip, peer_chip)
+    row_of = lax.broadcasted_iota(jnp.int32, (rows_dev, width), 0)
     for step in range(steps):
-        update_out[step] = acc[step * rows_dev : (step + 1) * rows_dev]
-    for copy in pending:
+        update = acc[step * rows_dev : (step + 1) * rows_dev]
+        update = jnp.where(row_of < live_ref[:, step : step + 1], update, 0.0)
+        out_ref[step] = (tokens_ref[step].astype(F32) + update).astype(BF16)
+    for i in range(nc):
+        source, target, recv, to = window_copy(i)
+
+        @pl.when(to != me)
+        def _():
+            rcopy(source, target, win_s.at[i], recv, {"expert": to}).wait_send()
+
+    for d in range(na):
+        at_distance(d, x_sent)
+    for copy in h_sent:
         copy.wait_send()
+    rcopy(r_p, r_pr, p_s.at[0], p_r.at[0], partner).wait_send()
+    for at in range(na):
+        rcopy(r_y.at[at], r_yr.at[at], y_s.at[at], y_r.at[at, 0], across).wait_send()
+
+        @pl.when(a != at)
+        def _():
+            rcopy(r_z.at[at], r_zr.at[0, at], z_s.at[at], z_r.at[0, at, 0], across).wait_send()
 
 
 def per_device(
@@ -505,9 +673,11 @@
     vmem = pltpu.VMEM
     whole = pl.BlockSpec(memory_space=pltpu.VMEM)
     anywhere = pl.BlockSpec(memory_space=pl.ANY)
-    update = pl.pallas_call(
-        functools.partial(layer_kernel, n, EXPERTS, group, chunk, window),
-        out_shape=jax.ShapeDtypeStruct(tokens.shape, F32),
+    x_chunk = chunk if nc <= EXPERTS else half
+    x_count = half // x_chunk
+    return pl.pallas_call(
+        functools.partial(layer_kernel, n, EXPERTS, group, chunk, window, x_chunk),
+        out_shape=jax.ShapeDtypeStruct(tokens.shape, BF16),
         in_specs=[whole] * 5 + [anywhere] * 4,
         out_specs=whole,
         scratch_shapes=[
@@ -515,10 +685,12 @@
             vmem((2, rows, wide), F32),
             vmem((rows, wide), F32),
             vmem((2, total, wide), BF16),
+            vmem((nc, pair, window), BF16),
             vmem((model_width, 2 * units), BF16),
             vmem((units, model_width), BF16),
             vmem((window, s_wide), BF16),
             vmem((fb, s_units), BF16),
+            vmem((total, max(2 * units, chunk)), F32),
             vmem((total, units), BF16),
             vmem((2, total, s_units), F32),
             vmem((total, s_units), BF16),
@@ -532,22 +704,23 @@
             vmem((nc, pair, fb), BF16),
             vmem((2, nc, rows, fb), F32),
             vmem((nc, rows, fb), F32),
-            vmem((total, chunk), F32),
             vmem((chunks, total, chunk), BF16),
             vmem((chunks, total, chunk), BF16),
-            vmem((chunks, y_rows, chunk), BF16),
-            vmem((chunks, y_rows, chunk), BF16),
-            vmem((chunks, na, pair, chunk), BF16),
-            vmem((chunks, na, pair, chunk), BF16),
-            vmem((chunks, y_rows, chunk), F32),
-            vmem((2, rows, half), F32),
-            vmem((rows, half), F32),
-            dma((14,)),
+            vmem((na, chunks, pair, chunk), BF16),
+            vmem((na, chunks, pair, chunk), BF16),
+            vmem((na, chunks, pair, chunk), BF16),
+            vmem((2, na, chunks, pair, chunk), BF16),
+            vmem((na, chunks, pair, chunk), F32),
+            vmem((2, chunks, rows, chunk), F32),
+            vmem((chunks, rows, chunk), F32),
+            dma((2 * x_count + 6,)),
             dma((2,)),
-            dma((na,)),
+            dma((nc,)),
+            dma((nc,)),
+            dma((2, na)),
             dma((na,)),
             dma((nc,)),
-            dma((2, nc)),
+            dma((2, nc, x_count)),
             dma((na,)),
             dma((na,)),
             dma((nc,)),
@@ -558,13 +731,14 @@
             dma((na,)),
             dma((nc,)),
             dma((nc,)),
+            dma((1,)),
             dma((chunks,)),
-            dma((chunks,)),
-            dma((chunks,)),
-            dma((chunks,)),
-            dma((chunks, na)),
-            dma((chunks, na)),
-            dma((4,)),
+            dma((na,)),
+            dma((na, chunks)),
+            dma((na,)),
+            dma((2, na, chunks)),
+            dma((2,)),
+            dma((2, chunks)),
         ],
         compiler_params=pltpu.CompilerParams(
             collective_id=0, has_side_effects=True, vmem_limit_bytes=67_043_328
@@ -580,9 +754,6 @@
         shared_gate_up,
         jnp.swapaxes(shared_down, 1, 2),
     )
-    live = jnp.arange(row_count, dtype=jnp.int32)[None, :] < live_rows
-    update = jnp.where(live[:, :, None], update, 0.0)
-    return (tokens.astype(F32) + update).astype(BF16)
 
 
 def solution(mesh):

time: 63 us -> 60.2 us (0.956); the launches traced: 62.9 us -> 59.2 us
  other arithmetic: 3.01 us -> 0 us
  Pallas kernels: 59.9 us -> 57.6 us
  local copies, waits for them, and re-layouts: 0 us -> 1.59 us
    pallas_call x1, Pallas kernels: 59.9 us -> 57.6 us  [per_device(): pl.pallas_call(functools.partial(layer_kernel, n, EXPERTS, group, chunk,...]
    convert_element_type x1 -> x0, other arithmetic: 1.77 us -> none  [per_device(): return (tokens.astype(F32) + update).astype(BF16)]
    unnamed x0 -> x1, local copies, waits for them, and re-layouts: none -> 1.59 us
    lt x1 -> x0, other arithmetic: 1.24 us -> none  [per_device(): live = jnp.arange(row_count, dtype=jnp.int32)[None, :] < live_rows]
where the time goes in v1:
time: 60.2 us; the launch traced here: 59.2 us
  Pallas kernels  57.6 us (96%)
  local copies, waits for them, and re-layouts  1.59 us (3%)
    pallas_call x1, Pallas kernels, per_device(): pl.pallas_call(functools.partial(layer_kernel, n, EXPERTS, group, chunk,...  57.6 us
    unnamed x1, local copies, waits for them, and re-layouts  1.59 us

profile of v1, /device:TPU:0, one launch (start us, length us, event | category | flops | bytes accessed | tf_op | source)
XLA Modules:
  0.0 59.2 jit_solution(5294120457608337276)
XLA Ops:
  0.0 57.6 %shard_map.91 = bf16[2,4,7168]{2,1,0:T(4,128)(2,1)} custom-call(bf16[2,4,7168]{2,1,0:T(4,128)(2,1)} %tokens_ref.1, s32[1,2]{1,0:T(1,128)} %bitcast.3, s32[1,2,4,8]{3,2,1,0:T(4,128)} %ids_ref.1, f32[1,2,4,8]{3,2,1,0:T(4,128)} %gates_ref.1, f32[1,7168]{1,0:T(1,128)} %gain_ref.1, bf16[1,1,7168,2048]{3,2,1,0:T(8,128)(2,1)} %gate_up_hbm.1, ...), custom_call_target="tpu_custom_call" | custom-call | tf_op jit(solution)/shard_map/pallas_call | solution.py:678
  57.6 1.6 %copy.11 = bf16[2,4,7168]{2,1,0:T(4,128)(2,1)} copy(bf16[2,4,7168]{2,1,0:T(4,128)(2,1)} %shard_map.91) | data formatting | bytes 229376

commit v2 on v1

v2 whole, which is shorter than its diff:
```python
import functools

import jax
import jax.numpy as jnp
from jax import lax
from jax.experimental import pallas as pl
from jax.experimental.pallas import tpu as pltpu
from jax.sharding import PartitionSpec as P

EXPERTS = 16
EPSILON = 1e-06
LANES = 128
X_TURNED = 3
R_TURNED = 2
GROUPED = 2
AT_PROJECT = 4
AT_ACROSS = 10
BF16 = jnp.bfloat16
F32 = jnp.float32


def dotted(left, right):
    return jnp.dot(left, right, preferred_element_type=F32)


def dotted_nt(left, right):
    return lax.dot_general(left, right, (((1,), (1,)), ((), ())), preferred_element_type=F32)


def layer_kernel(
    n,
    experts,
    group,
    chunk,
    window,
    x_chunk,
    x_turned,
    r_turned,
    tokens_ref,
    live_ref,
    ids_ref,
    gates_ref,
    gain_ref,
    gate_up_hbm,
    down_hbm,
    shared_up_hbm,
    shared_down_hbm,
    out_ref,
    acc,
    own_n,
    peer_n,
    x_all,
    x_win,
    gate_up,
    down,
    shared_up,
    shared_down,
    up_acc,
    hidden,
    sh_part,
    sh_send,
    sh_peer,
    sh_z,
    sh_zr,
    sh_hidden,
    so_send,
    so_recv,
    r_p,
    r_pr,
    r_y,
    r_yr,
    r_z,
    r_zr,
    r_cr,
    cross,
    keep,
    res,
    res_r,
    w_sem,
    n_sem,
    win_s,
    win_r,
    xz_s,
    xc_s,
    xy_s,
    xp_s,
    x_r,
    xp_r,
    h_sem,
    sp_sem,
    sz_sem,
    so_sem,
    p_s,
    p_r,
    c_s,
    c_r,
    y_s,
    y_r,
    z_s,
    z_r,
    l_s,
    l_r,
):
    nc = n // 2
    na = nc // 2
    me = lax.axis_index("expert")
    barrier = pltpu.get_barrier_semaphore()
    for d in range(1, n):
        pl.semaphore_signal(
            barrier,
            inc=1,
            device_id={"expert": lax.rem(me + d, n)},
            device_id_type=pl.DeviceIdType.MESH,
        )
    c = lax.rem(me, 2)
    chip = lax.div(me, 2)
    b = lax.rem(chip, 2)
    a = lax.div(chip, 2)
    slot = b * na + a
    oc = 1 - c
    steps, rows_dev, width = tokens_ref.shape
    half = width // 2
    rows = steps * rows_dev
    pair = 2 * rows
    total_rows = nc * pair
    y_rows = na * pair
    units = down.shape[0]
    s_units = sh_part.shape[2]
    fb = shared_down.shape[0]
    x_count = half // x_chunk
    chunks = half // chunk

    def dev(a_at, b_at, c_at):
        return {"expert": (2 * a_at + b_at) * 2 + c_at}

    partner = dev(a, b, oc)
    across = dev(a, 1 - b, c)
    below = dev(a - 1, b, c)
    above = dev(a + 1, b, c)

    def rcopy(src, dst, send, recv, to):
        return pltpu.make_async_remote_copy(
            src_ref=src,
            dst_ref=dst,
            send_sem=send,
            recv_sem=recv,
            device_id=to,
            device_id_type=pl.DeviceIdType.MESH,
        )

    def a_of(d):
        return lax.rem(a + d, na)

    def block(at):
        return pl.ds(pl.multiple_of(at * pair, pair), pair)

    loads = []
    offset = lax.rem(me, nc) * fb
    start = lax.div(offset, LANES) * LANES
    inner = pl.multiple_of(offset - start, 16)
    loads.append(
        pltpu.make_async_copy(
            shared_up_hbm.at[0], shared_up.at[pl.ds(inner, fb)], w_sem.at[0]
        )
    )
    for at in range(x_count):
        for side in range(2):
            piece = pl.ds(side * half + at * x_chunk, x_chunk)
            loads.append(
                pltpu.make_async_copy(
                    gate_up_hbm.at[0, 0, piece], gate_up.at[piece], w_sem.at[3 + at]
                )
            )
    loads.append(pltpu.make_async_copy(down_hbm.at[0, 0], down, w_sem.at[1]))
    down_load = loads[-1]
    loads.append(pltpu.make_async_copy(shared_down_hbm.at[0], shared_down, w_sem.at[2]))
    shared_down_load = loads[-1]

    def gate_up_wait(k):
        view = gate_up.at[pl.ds(0, 2 * x_chunk)]
        pltpu.make_async_copy(view, view, w_sem.at[3 + k]).wait()

    shared_up[...] = jnp.zeros_like(shared_up)

    for load in loads:
        load.start()

    lane = lax.broadcasted_iota(jnp.int32, (rows_dev, LANES), 1)
    row_at = lax.broadcasted_iota(jnp.int32, (rows_dev, LANES), 0)
    of_lane = lane & (experts - 1)
    level = lax.div(lane, experts)
    gain = gain_ref[...]
    for step in range(steps):
        h = tokens_ref[step].astype(F32)
        scaling = lax.rsqrt(jnp.mean(h * h, axis=-1, keepdims=True) + EPSILON)
        normed = (h * scaling * gain).astype(BF16).astype(F32)
        ids = ids_ref[0, step]
        gates = gates_ref[0, step]
        dense = jnp.zeros((rows_dev, LANES), F32)
        for k in range(ids.shape[1]):
            dense = dense + jnp.where(ids[:, k : k + 1] == of_lane, gates[:, k : k + 1], 0.0)
        dense = jnp.where(row_at < live_ref[:, step : step + 1], dense, 0.0)
        high = dense.astype(BF16).astype(F32)
        rest = dense - high
        mid = rest.astype(BF16).astype(F32)
        low = rest - mid
        coded = jnp.where(
            level == 0, high, jnp.where(level == 1, mid, jnp.where(level == 2, low, 0.0))
        )
        at = slice(step * rows_dev, (step + 1) * rows_dev)
        for side in range(2):
            own_n[side, at, :half] = normed[:, side * half : (side + 1) * half]
            own_n[side, at, half:] = coded

    pl.semaphore_wait(barrier, n - 1)

    swap = rcopy(own_n.at[oc], peer_n, n_sem.at[0], n_sem.at[1], partner)
    swap.start()
    swap.wait()
    mine = own_n[c]
    theirs = peer_n[...]
    first = jnp.where(c == 0, mine, theirs)
    second = jnp.where(c == 0, theirs, mine)
    x_all[c, block(slot)] = jnp.concatenate([first, second], axis=0).astype(BF16)

    def window_copy(i):
        lo = i * fb // LANES * LANES
        source = x_all.at[c, block(slot), pl.ds(lo, window)]
        return source, x_win.at[slot], win_r.at[0], c * nc + i

    def x_view(side, at, k):
        wide = x_chunk + (LANES if k == x_count - 1 else 0)
        return x_all.at[side, block(at), pl.ds(k * x_chunk, wide)]

    def x_push(at, k, send, to):
        view = x_view(c, at, k)
        rcopy(view, view, send, x_r.at[at, k], to).start()

    def x_twin(at, k):
        view = x_view(c, at, k)
        rcopy(view, view, xp_s.at[0], xp_r.at[k], partner).start()

    def x_arrived(at, k):
        view = x_view(c, at, k)
        rcopy(view, view, xp_s.at[0], x_r.at[at, k], partner).wait_recv()

    gate_down = lax.rem(a, 2) == 1
    gate_up_way = lax.rem(na - 1 - a, 2) == 1

    def x_steps(d, down_line, up_line):
        for way, line, gate in ((0, down_line, gate_down), (1, up_line, gate_up_way)):
            for step in (1, 2):
                if line:
                    inside = a >= step if way == 0 else a < na - step
                    goes = inside if d == 0 and step == 1 else inside & gate
                    yield way, step, goes, dev(a - step if way == 0 else a + step, b, c)

    def at_distance(d, body):
        if d == 0:
            body(a, True, True)
            return

        @pl.when(a + d < na)
        def _():
            body(a + d, True, False)

        @pl.when(a - d >= 0)
        def _():
            body(a - d, False, True)

    def x_along(d, k, gates=True):
        if not 0 <= k < x_count:
            return

        def one(source, down_line, up_line):
            at = b * na + source

            def handle():
                if d:
                    x_arrived(at, k)
                for way, step, goes, to in x_steps(d, down_line, up_line):

                    @pl.when(goes)
                    def _():
                        x_push(at, k, xz_s.at[way, step - 1, source], to)

                if d != 1 or k >= x_turned:
                    x_push(at, k, xy_s.at[source], across)
                x_twin(at, k)

            if d < 2:
                handle()
            else:
                gate = gate_down if down_line else gate_up_way
                pl.when(gate if gates else jnp.logical_not(gate))(handle)

        at_distance(d, one)

    def x_crossed(d, k):
        if not 0 <= k < x_count:
            return

        def one(source, down_line, up_line):
            at = (1 - b) * na + source
            x_arrived(at, k)
            if d == 0 and k < x_turned:
                for way, inside, to in ((0, a > 0, below), (1, a < na - 1, above)):

                    @pl.when(inside)
                    def _():
                        x_push(at, k, xc_s.at[way], to)

            x_twin(at, k)

        at_distance(d, one)

    def x_sent(d):
        def sent(sem, lo=0, hi=half + LANES):
            if lo < hi:
                view = x_all.at[c, block(0), pl.ds(lo, hi - lo)]
                rcopy(view, view, sem, x_r.at[0, 0], partner).wait_send()

        turned = half + LANES if x_turned == x_count else x_turned * x_chunk

        def one(source, down_line, up_line):
            for way, step, goes, _ in x_steps(d, down_line, up_line):

                @pl.when(goes)
                def _():
                    sent(xz_s.at[way, step - 1, source])

            if d == 0:
                for way, inside in ((0, a > 0), (1, a < na - 1)):

                    @pl.when(inside)
                    def _():
                        sent(xc_s.at[way], 0, turned)

            sent(xy_s.at[source], turned if d == 1 else 0)

        at_distance(d, one)

    s_half = s_units // 2

    def shared_project():
        loads[0].wait()
        rcopy(x_win, x_win, win_s.at[0], win_r.at[0], partner).wait_recv()
        features = x_win[...].reshape(total_rows, window)
        for side in range(2):
            for kind in range(2):
                cols = slice(kind * s_units + side * s_half, kind * s_units + (side + 1) * s_half)
                sh_part[side, :, kind * s_half : (kind + 1) * s_half] = dotted(
                    features, shared_up[:, cols]
                )
        sh_send[...] = sh_part[oc].astype(BF16)
        copy = rcopy(sh_send, sh_peer, sp_sem.at[0], sp_sem.at[1], partner)
        copy.start()
        return copy

    y_own = pl.ds(pl.multiple_of(b * y_rows, y_rows), y_rows)
    y_other = pl.ds(pl.multiple_of((1 - b) * y_rows, y_rows), y_rows)

    def shared_spread(copy):
        copy.wait()
        sh_part[0] = sh_part[c] + sh_peer[...].astype(F32)
        sh_z[...] = sh_part[0].astype(BF16).reshape(nc, pair, s_units)
        for d in range(1, nc):
            other = lax.rem(chip + d, nc)
            rcopy(
                sh_z.at[lax.rem(other, 2) * na + lax.div(other, 2)],
                sh_zr.at[d - 1],
                sz_sem.at[0],
                sz_sem.at[1],
                {"expert": other * 2 + c},
            ).start()

    others = pl.ds(0, (nc - 1) * pair)

    def shared_active():
        rcopy(sh_zr, sh_zr, sz_sem.at[0], sz_sem.at[1], partner).wait()
        total = sh_part[0, block(slot)]
        for d in range(1, nc):
            total = total + sh_zr[d - 1].astype(F32)
        sh_hidden[c, block(slot)] = (
            jax.nn.silu(total[:, :s_half]) * total[:, s_half:]
        ).astype(BF16)
        view = sh_hidden.at[c, block(slot)]
        for d in range(1, nc):
            to = {"expert": lax.rem(chip + d, nc) * 2 + c}
            rcopy(view, view, h_sem.at[0], h_sem.at[1], to).start()

    def shared_twin():
        view = sh_hidden.at[c, others]
        rcopy(view, view, h_sem.at[0], h_sem.at[1], partner).wait()
        view = sh_hidden.at[c]
        rcopy(view, view, h_sem.at[2], h_sem.at[3], partner).start()

    def shared_last():
        view = sh_hidden.at[c]
        rcopy(view, view, h_sem.at[2], h_sem.at[3], partner).wait()
        shared_down_load.wait()
        cols = dotted_nt(sh_hidden[0], shared_down[:, :s_half]) + dotted_nt(
            sh_hidden[1], shared_down[:, s_half:]
        )
        cols = cols.reshape(n, rows, fb).astype(BF16)
        for at in range(n):
            owner = 4 * (at // 2 % na) + 2 * (at // 2 // na) + at % 2
            so_send[lax.rem(owner - me + n, n)] = cols[at]
        for d in range(1, n):
            to = {"expert": lax.rem(me + d, n)}
            rcopy(so_send.at[d], so_recv.at[n - d], so_sem.at[0], so_sem.at[1], to).start()
        so_recv[0] = so_send[0]

    def shared_collect():
        view = so_recv.at[pl.ds(1, n - 1)]
        rcopy(view, view, so_sem.at[0], so_sem.at[1], partner).wait()

    def up_term(k, cols):
        at = k * x_chunk
        return dotted(x_all[0, :, at : at + x_chunk], gate_up[at : at + x_chunk, cols]) + dotted(
            x_all[1, :, at : at + x_chunk], gate_up[half + at : half + at + x_chunk, cols]
        )

    tile = min(256, units)

    def up_part(k):
        wide = x_chunk + (LANES if k == x_count - 1 else 0)
        view = x_all.at[oc, :, pl.ds(k * x_chunk, wide)]
        rcopy(view, view, xp_s.at[0], xp_r.at[k], partner).wait_recv()
        gate_up_wait(k)
        if k < x_count - 1:
            for at in range(2 * units // tile):
                cols = slice(at * tile, (at + 1) * tile)
                if k == 0:
                    up_acc[:, cols] = up_term(k, cols)
                else:
                    up_acc[:, cols] += up_term(k, cols)
            return
        for at in range(units // tile):
            gate_cols = slice(at * tile, (at + 1) * tile)
            up_cols = slice(units + at * tile, units + (at + 1) * tile)
            gate = up_term(k, gate_cols)
            up = up_term(k, up_cols)
            if k:
                gate = gate + up_acc[:, gate_cols]
                up = up + up_acc[:, up_cols]
            hidden[:, gate_cols] = (jax.nn.silu(gate) * up).astype(BF16)

    for i in range(nc):
        source, target, recv, to = window_copy(i)

        @pl.when(to != me)
        def _():
            rcopy(source, target, win_s.at[0], recv, {"expert": to}).start()

        @pl.when(to == me)
        def _():
            pltpu.make_async_copy(source, target, recv).start()

    for k in range(x_count):
        x_along(0, k)
    def gate_lag(d):
        return 3 * ((d - 1) // 2)

    def leaf_lag(d):
        return 0 if d < 2 else 3 * ((d - 2) // 2) + 3

    last_lag = leaf_lag(na - 1) + 4
    up_lag = last_lag + 2
    count = x_count + up_lag
    shared_copy = None
    for i in range(count):
        for d in range(1, na):
            x_along(d, i - gate_lag(d))
        x_crossed(0, i)
        for d in range(2, na):
            x_along(d, i - leaf_lag(d), False)
        if i == min(AT_PROJECT, count - 4):
            shared_copy = shared_project()
        if i == min(AT_ACROSS, count - 3):
            shared_spread(shared_copy)
        for d in range(1, na - 1):
            x_crossed(d, i - leaf_lag(d) - 4)
        x_crossed(na - 1, i - last_lag)
        if i >= up_lag:
            up_part(i - up_lag)

    expert = lax.div(me, group)
    codes = x_all[0, :, half:].astype(F32)
    wide = lax.broadcasted_iota(jnp.int32, (total_rows, LANES), 1) & (experts - 1)
    weight = jnp.sum(jnp.where(wide == expert, codes, 0.0), axis=1, keepdims=True)

    down_load.wait()

    def product(side, group):
        wide = chunk * len(group)
        cols = pl.ds(pl.multiple_of(side * half + group[0] * chunk, LANES), wide)
        return dotted(hidden[...], down[:, cols]) * weight

    def send_partner(group):
        sums = product(oc, group).astype(BF16)
        for place, j in enumerate(group):
            r_p[j] = sums[:, place * chunk : (place + 1) * chunk]
        for j in group:
            rcopy(r_p.at[j], r_pr.at[j], p_s.at[0], p_r.at[j], partner).start()

    def send_across(at, j):
        rcopy(r_y.at[at, j], r_yr.at[at, j], y_s.at[at], y_r.at[at, j], across).start()

    cross_rows = block((1 - b) * na + a)

    def own_part(group):
        up_acc[:, : chunk * len(group)] = product(c, group)
        for j in group:
            rcopy(r_p.at[j], r_pr.at[j], p_s.at[0], p_r.at[j], partner).wait_recv()
        for place, j in enumerate(group):
            cols = slice(place * chunk, (place + 1) * chunk)
            other = (up_acc[y_other, cols] + r_pr[j, y_other].astype(F32)).astype(BF16)
            for at in range(na):
                r_y[at, j] = other[at * pair : (at + 1) * pair]
        for place, j in enumerate(group):
            for d in range(na - 1, 1, -1):
                at_distance(d, lambda at, up_line, down_line: send_across(at, j))

            def beside(at, up_line, down_line):
                way, to = (1, above) if up_line else (0, below)
                rcopy(r_y.at[at, j], r_cr.at[way, j], c_s.at[way], c_r.at[way, j], to).start()

            if j < r_turned:
                at_distance(1, beside)
        for place, j in enumerate(group):
            cols = slice(place * chunk, (place + 1) * chunk)
            cross[j] = up_acc[cross_rows, cols] + r_pr[j, cross_rows].astype(F32)
            here = up_acc[y_own, cols] + r_pr[j, y_own].astype(F32)
            for at in range(na):
                keep[at, j] = here[at * pair : (at + 1) * pair]

    def join(j):
        for way, inside in ((1, a > 0), (0, a < na - 1)) if j < r_turned else ():

            @pl.when(inside)
            def _():
                view = r_cr.at[way, j]
                rcopy(view, view, c_s.at[0], c_r.at[way, j], across).wait_recv()
                cross[j] = cross[j] + r_cr[way, j].astype(F32)

        r_y[a, j] = cross[j].astype(BF16)
        send_across(a, j)

    def y_arrived(at, j):
        rcopy(r_y.at[at, j], r_yr.at[at, j], y_s.at[at], y_r.at[at, j], across).wait_recv()

    def z_place(step, place):
        if step == 1 or na > 4:
            return (step - 1) * (na + 1) + place
        return na + 1 + (place is na)

    def z_add(step, place, at, j):
        index = z_place(step, place)
        view = r_zr.at[index, j]
        rcopy(view, view, z_s.at[0], z_r.at[index, j], across).wait_recv()
        keep[at, j] = keep[at, j] + r_zr[index, j].astype(F32)

    def gate_even(up_line):
        return lax.rem(na - 1 - a if up_line else a, 2) == 0

    def leaf(up_line):
        return jnp.logical_not(gate_even(up_line))

    def z_pass(d, j, only=None):
        def one(at, up_line, down_line):
            if only is None:
                forward(at, up_line)
            else:
                pl.when(only(up_line))(lambda: forward(at, up_line))

        def forward(at, up_line):
            if d > 1 or j >= r_turned:
                y_arrived(at, j)
                keep[at, j] = keep[at, j] + r_yr[at, j].astype(F32)
            for step in (1, 2):
                if d + step < na:

                    @pl.when(gate_even(up_line) & (a >= step if up_line else a < na - step))
                    def _():
                        z_add(step, at, at, j)

            r_z[at, j] = keep[at, j].astype(BF16)
            last = na if not up_line else at

            def send(hop, place):
                to = dev(a + hop if up_line else a - hop, b, c)
                index = z_place(hop, place)
                rcopy(
                    r_z.at[at, j], r_zr.at[index, j], z_s.at[0], z_r.at[index, j], to
                ).start()

            if d == 1:
                send(1, last)
            else:
                even = gate_even(up_line)
                pl.when(even)(lambda: send(2, last if d == 2 else at))
                pl.when(jnp.logical_not(even))(lambda: send(1, at))

        at_distance(d, one)

    def collect(j):
        y_arrived(a, j)
        keep[a, j] = keep[a, j] + r_yr[a, j].astype(F32)
        for step in (1, 2):
            for place, inside, up_line in ((a, a >= step, True), (na, a < na - step, False)):
                if step == 2:
                    inside = inside & gate_even(up_line)

                @pl.when(inside)
                def _():
                    z_add(step, place, a, j)

        total = keep[a, j]
        res[0, j] = total[:rows]
        res[1, j] = total[rows:]
        rcopy(res.at[oc, j], res_r.at[j], l_s.at[0], l_r.at[j], partner).start()

    groups = [tuple(range(j, min(j + GROUPED, chunks))) for j in range(0, chunks, GROUPED)]
    send_partner(groups[0])
    for at, group in enumerate(groups):
        if at + 1 < len(groups):
            send_partner(groups[at + 1])
        own_part(group)
        for j in group:
            if j < r_turned:
                z_pass(1, j, leaf)
    shared_active()
    for j in range(r_turned, chunks):
        at_distance(1, lambda at, up_line, down_line: send_across(at, j))
    for j in range(chunks):
        join(j)
    for d in range(na - 1, 2, -1):
        for j in range(chunks):
            z_pass(d, j)
    if na > 2:
        for j in range(chunks):
            z_pass(2, j, leaf)
    shared_twin()
    if na > 2:
        for j in range(chunks):
            z_pass(2, j, gate_even)
    shared_last()
    for j in range(chunks):
        z_pass(1, j, gate_even if j < r_turned else None)
    for j in range(chunks):
        collect(j)
    shared_collect()
    for j in range(chunks):
        rcopy(res.at[oc, j], res_r.at[j], l_s.at[0], l_r.at[j], partner).wait_recv()
        own_cols = pl.ds(pl.multiple_of(c * half + j * chunk, LANES), chunk)
        other_cols = pl.ds(pl.multiple_of(oc * half + j * chunk, LANES), chunk)
        acc[:, own_cols] = res[c, j]
        acc[:, other_cols] = res_r[j]
    for at in range(n):
        cols = slice(at * fb, (at + 1) * fb)
        acc[:, cols] = acc[:, cols] + so_recv[lax.rem(at - me + n, n)].astype(F32)
    row_of = lax.broadcasted_iota(jnp.int32, (rows_dev, width), 0)
    for step in range(steps):
        update = acc[step * rows_dev : (step + 1) * rows_dev]
        update = jnp.where(row_of < live_ref[:, step : step + 1], update, 0.0)
        out_ref[step] = (tokens_ref[step].astype(F32) + update).astype(BF16)
    @pl.when(lax.div(me, nc) == c)
    def _():
        view = x_win.at[pl.ds(0, nc - 1)]
        rcopy(view, view, win_s.at[0], win_r.at[0], partner).wait_send()

    @pl.when(lax.div(me, nc) != c)
    def _():
        rcopy(x_win, x_win, win_s.at[0], win_r.at[0], partner).wait_send()

    for d in range(na):
        x_sent(d)
    view = x_all.at[c]
    rcopy(view, view, xp_s.at[0], xp_r.at[0], partner).wait_send()
    rcopy(r_p, r_pr, p_s.at[0], p_r.at[0], partner).wait_send()
    for d in range(na):
        first = r_turned if d == 1 else 0

        def y_sent(at, up_line, down_line):
            view = r_y.at[at, pl.ds(first, chunks - first)]
            rcopy(view, view, y_s.at[at], y_r.at[0, 0], across).wait_send()

        if first < chunks:
            at_distance(d, y_sent)
    for way, inside in ((0, a > 0), (1, a < na - 1)) if r_turned else ():

        @pl.when(inside)
        def _():
            view = r_cr.at[way, pl.ds(0, r_turned)]
            rcopy(view, view, c_s.at[way], c_r.at[0, 0], across).wait_send()

    view = r_z.at[pl.ds(0, na - 1)]
    rcopy(view, view, z_s.at[0], z_r.at[0, 0], across).wait_send()
    view = res.at[oc]
    rcopy(view, res_r, l_s.at[0], l_r.at[0], partner).wait_send()


def per_device(
    tokens,
    live_rows,
    expert_ids,
    gate_weights,
    norm_gain,
    expert_gate_up,
    expert_down,
    shared_gate_up,
    shared_down,
):
    step_count, row_count, model_width = tokens.shape
    n = lax.axis_size("expert")
    group = n // EXPERTS
    units = expert_down.shape[2]
    fb, s_wide = shared_gate_up.shape[1:]
    s_units = s_wide // 2
    nc = n // 2
    na = nc // 2
    half = model_width // 2
    rows = step_count * row_count
    pair = 2 * rows
    total = nc * pair
    y_rows = na * pair
    wide = half + LANES
    chunk = next(size for size in (512, 256, 128) if half % size == 0)
    chunks = half // chunk
    span = next(size for size in (128, 64, 32, 16) if fb % size == 0)
    window = -(-(fb + LANES - span) // LANES) * LANES
    dma = pltpu.SemaphoreType.DMA
    vmem = pltpu.VMEM
    whole = pl.BlockSpec(memory_space=pltpu.VMEM)
    anywhere = pl.BlockSpec(memory_space=pl.ANY)
    x_chunk = chunk if nc <= EXPERTS else half
    x_count = half // x_chunk
    x_turned = min(X_TURNED, x_count)
    r_turned = min(R_TURNED, chunks)
    z_places = 2 * na + 2 if na > 4 else na + 3
    return pl.pallas_call(
        functools.partial(layer_kernel, n, EXPERTS, group, chunk, window, x_chunk, x_turned, r_turned),
        out_shape=jax.ShapeDtypeStruct(tokens.shape, BF16),
        in_specs=[whole] * 5 + [anywhere] * 4,
        out_specs=whole,
        scratch_shapes=[
            vmem((rows, model_width), F32),
            vmem((2, rows, wide), F32),
            vmem((rows, wide), F32),
            vmem((2, total, wide), BF16),
            vmem((nc, pair, window), BF16),
            vmem((model_width, 2 * units), BF16),
            vmem((units, model_width), BF16),
            vmem((window, s_wide), BF16),
            vmem((fb, s_units), BF16),
            vmem((total, max(2 * units, GROUPED * chunk)), F32),
            vmem((total, units), BF16),
            vmem((2, total, s_units), F32),
            vmem((total, s_units), BF16),
            vmem((total, s_units), BF16),
            vmem((nc, pair, s_units), BF16),
            vmem((nc - 1, pair, s_units), BF16),
            vmem((2, total, s_units // 2), BF16),
            vmem((n, rows, fb), BF16),
            vmem((n, rows, fb), BF16),
            vmem((chunks, total, chunk), BF16),
            vmem((chunks, total, chunk), BF16),
            vmem((na, chunks, pair, chunk), BF16),
            vmem((na, chunks, pair, chunk), BF16),
            vmem((na, chunks, pair, chunk), BF16),
            vmem((z_places, chunks, pair, chunk), BF16),
            vmem((2, chunks, pair, chunk), BF16),
            vmem((chunks, pair, chunk), F32),
            vmem((na, chunks, pair, chunk), F32),
            vmem((2, chunks, rows, chunk), F32),
            vmem((chunks, rows, chunk), F32),
            dma((3 + x_count,)),
            dma((2,)),
            dma((1,)),
            dma((1,)),
            dma((2, 2, na)),
            dma((2,)),
            dma((na,)),
            dma((1,)),
            dma((nc, x_count)),
            dma((x_count,)),
            dma((4,)),
            dma((2,)),
            dma((2,)),
            dma((2,)),
            dma((1,)),
            dma((chunks,)),
            dma((2,)),
            dma((2, chunks)),
            dma((na,)),
            dma((na, chunks)),
            dma((1,)),
            dma((z_places, chunks)),
            dma((1,)),
            dma((chunks,)),
        ],
        compiler_params=pltpu.CompilerParams(
            collective_id=0, has_side_effects=True, vmem_limit_bytes=67_043_328
        ),
    )(
        tokens,
        live_rows.T,
        expert_ids,
        gate_weights,
        norm_gain,
        expert_gate_up,
        expert_down,
        shared_gate_up,
        jnp.swapaxes(shared_down, 1, 2),
    )


def solution(mesh):
    placed = (
        P(None, ("parts", "expert"), None),
        P(None, ("parts", "expert")),
        P(None, None, ("parts", "expert"), None),
        P(None, None, ("parts", "expert"), None),
        P(),
        P(None, "expert", None, None),
        P(None, "expert", None, None),
        P(None, "expert", None),
        P(None, None, "expert"),
    )
    return jax.shard_map(
        per_device,
        mesh=mesh,
        in_specs=placed,
        out_specs=P(None, ("parts", "expert"), None),
        check_vma=False,
    )
```

time: 60.2 us -> 52.5 us (0.87); the launches traced: 59.2 us -> 52.2 us
  Pallas kernels: 57.6 us -> 50.6 us
    pallas_call x1, Pallas kernels: 57.6 us -> 50.6 us  [per_device(): pl.pallas_call(functools.partial(layer_kernel, n, EXPERTS, group, chunk,...]
where the time goes in v2:
time: 52.5 us; the launch traced here: 52.2 us
  Pallas kernels  50.6 us (96%)
  local copies, waits for them, and re-layouts  1.59 us (3%)
    pallas_call x1, Pallas kernels, per_device(): pl.pallas_call(functools.partial(layer_kernel, n, EXPERTS, group, chunk,...  50.6 us
    unnamed x1, local copies, waits for them, and re-layouts  1.59 us

profile of v2, /device:TPU:0, one launch (start us, length us, event | category | flops | bytes accessed | tf_op | source)
XLA Modules:
  0.0 52.2 jit_solution(15955834048858477406)
XLA Ops:
  0.0 50.6 %shard_map.91 = bf16[2,4,7168]{2,1,0:T(4,128)(2,1)} custom-call(bf16[2,4,7168]{2,1,0:T(4,128)(2,1)} %tokens_ref.1, s32[1,2]{1,0:T(1,128)} %bitcast.3, s32[1,2,4,8]{3,2,1,0:T(4,128)} %ids_ref.1, f32[1,2,4,8]{3,2,1,0:T(4,128)} %gates_ref.1, f32[1,7168]{1,0:T(1,128)} %gain_ref.1, bf16[1,1,7168,2048]{3,2,1,0:T(8,128)(2,1)} %gate_up_hbm.1, ...), custom_call_target="tpu_custom_call" | custom-call | tf_op jit(solution)/shard_map/pallas_call | solution.py:742
  50.6 1.6 %copy.11 = bf16[2,4,7168]{2,1,0:T(4,128)(2,1)} copy(bf16[2,4,7168]{2,1,0:T(4,128)(2,1)} %shard_map.91) | data formatting | bytes 229376

commit v3 on v2

--- a/solution.py
+++ b/solution.py
@@ -13,8 +13,8 @@
 X_TURNED = 3
 R_TURNED = 2
 GROUPED = 2
-AT_PROJECT = 4
-AT_ACROSS = 10
+AT_PROJECT = 8
+AT_ACROSS = 11
 BF16 = jnp.bfloat16
 F32 = jnp.float32
 
@@ -446,6 +446,8 @@
                 up = up + up_acc[:, up_cols]
             hidden[:, gate_cols] = (jax.nn.silu(gate) * up).astype(BF16)
 
+    for k in range(x_count):
+        x_along(0, k)
     for i in range(nc):
         source, target, recv, to = window_copy(i)
 
@@ -457,8 +459,6 @@
         def _():
             pltpu.make_async_copy(source, target, recv).start()
 
-    for k in range(x_count):
-        x_along(0, k)
     def gate_lag(d):
         return 3 * ((d - 1) // 2)
 
@@ -507,6 +507,7 @@
     def send_across(at, j):
         rcopy(r_y.at[at, j], r_yr.at[at, j], y_s.at[at], y_r.at[at, j], across).start()
 
+    far = jnp.where(2 * a >= na, 0, na - 1)
     cross_rows = block((1 - b) * na + a)
 
     def own_part(group):
@@ -519,8 +520,7 @@
             for at in range(na):
                 r_y[at, j] = other[at * pair : (at + 1) * pair]
         for place, j in enumerate(group):
-            for d in range(na - 1, 1, -1):
-                at_distance(d, lambda at, up_line, down_line: send_across(at, j))
+            send_across(far, j)
 
             def beside(at, up_line, down_line):
                 way, to = (1, above) if up_line else (0, below)
@@ -630,6 +630,15 @@
         for j in group:
             if j < r_turned:
                 z_pass(1, j, leaf)
+    for d in range(na - 2, 1, -1):
+
+        def send_rest(at, up_line, down_line):
+            @pl.when(at != far)
+            def _():
+                for j in range(chunks):
+                    send_across(at, j)
+
+        at_distance(d, send_rest)
     shared_active()
     for j in range(r_turned, chunks):
         at_distance(1, lambda at, up_line, down_line: send_across(at, j))

time: 52.5 us -> 49.9 us (0.950)
  Pallas kernels: 50.6 us -> 48.1 us
    pallas_call x1, Pallas kernels: 50.6 us -> 48.1 us  [per_device(): pl.pallas_call(functools.partial(layer_kernel, n, EXPERTS, group, chunk,...]
where the time goes in v3:
time: 49.9 us; the launch traced here: 49.7 us
  Pallas kernels  48.1 us (96%)
  local copies, waits for them, and re-layouts  1.59 us (3%)
    pallas_call x1, Pallas kernels, per_device(): pl.pallas_call(functools.partial(layer_kernel, n, EXPERTS, group, chunk,...  48.1 us
    unnamed x1, local copies, waits for them, and re-layouts  1.59 us

profile of v3, /device:TPU:0, one launch (start us, length us, event | category | flops | bytes accessed | tf_op | source)
XLA Modules:
  0.0 49.7 jit_solution(11514103122041489196)
XLA Ops:
  0.0 48.1 %shard_map.91 = bf16[2,4,7168]{2,1,0:T(4,128)(2,1)} custom-call(bf16[2,4,7168]{2,1,0:T(4,128)(2,1)} %tokens_ref.1, s32[1,2]{1,0:T(1,128)} %bitcast.3, s32[1,2,4,8]{3,2,1,0:T(4,128)} %ids_ref.1, f32[1,2,4,8]{3,2,1,0:T(4,128)} %gates_ref.1, f32[1,7168]{1,0:T(1,128)} %gain_ref.1, bf16[1,1,7168,2048]{3,2,1,0:T(8,128)(2,1)} %gate_up_hbm.1, ...), custom_call_target="tpu_custom_call" | custom-call | tf_op jit(solution)/shard_map/pallas_call | solution.py:751
  48.1 1.6 %copy.11 = bf16[2,4,7168]{2,1,0:T(4,128)(2,1)} copy(bf16[2,4,7168]{2,1,0:T(4,128)(2,1)} %shard_map.91) | data formatting | bytes 229376

commit v4 on v3

--- a/solution.py
+++ b/solution.py
@@ -10,7 +10,7 @@
 EXPERTS = 16
 EPSILON = 1e-06
 LANES = 128
-X_TURNED = 3
+X_TURNED = 0
 R_TURNED = 2
 GROUPED = 2
 AT_PROJECT = 8
@@ -80,8 +80,6 @@
     n_sem,
     win_s,
     win_r,
-    xz_s,
-    xc_s,
     xy_s,
     xp_s,
     x_r,
@@ -282,10 +280,10 @@
 
                     @pl.when(goes)
                     def _():
-                        x_push(at, k, xz_s.at[way, step - 1, source], to)
+                        x_push(at, k, xy_s.at[0], to)
 
                 if d != 1 or k >= x_turned:
-                    x_push(at, k, xy_s.at[source], across)
+                    x_push(at, k, xy_s.at[0], across)
                 x_twin(at, k)
 
             if d < 2:
@@ -308,37 +306,22 @@
 
                     @pl.when(inside)
                     def _():
-                        x_push(at, k, xc_s.at[way], to)
+                        x_push(at, k, xy_s.at[0], to)
 
             x_twin(at, k)
 
         at_distance(d, one)
 
-    def x_sent(d):
-        def sent(sem, lo=0, hi=half + LANES):
-            if lo < hi:
-                view = x_all.at[c, block(0), pl.ds(lo, hi - lo)]
-                rcopy(view, view, sem, x_r.at[0, 0], partner).wait_send()
-
-        turned = half + LANES if x_turned == x_count else x_turned * x_chunk
-
-        def one(source, down_line, up_line):
-            for way, step, goes, _ in x_steps(d, down_line, up_line):
-
-                @pl.when(goes)
-                def _():
-                    sent(xz_s.at[way, step - 1, source])
-
-            if d == 0:
-                for way, inside in ((0, a > 0), (1, a < na - 1)):
-
-                    @pl.when(inside)
-                    def _():
-                        sent(xc_s.at[way], 0, turned)
-
-            sent(xy_s.at[source], turned if d == 1 else 0)
-
-        at_distance(d, one)
+    def x_sent(at):
+        blocks = na
+        for step in (1, 2):
+            blocks += (at >= step) * (1 if step == 1 else at % 2)
+            blocks += (at < na - step) * (1 if step == 1 else (na - 1 - at) % 2)
+            if at % 2:
+                blocks += (na - 1 - at) * (at >= step)
+            if (na - 1 - at) % 2:
+                blocks += at * (at < na - step)
+        return blocks
 
     s_half = s_units // 2
 
@@ -492,6 +475,9 @@
 
     down_load.wait()
 
+    def paired(j):
+        return pl.ds(j, min(2, chunks - j))
+
     def product(side, group):
         wide = chunk * len(group)
         cols = pl.ds(pl.multiple_of(side * half + group[0] * chunk, LANES), wide)
@@ -502,18 +488,19 @@
         for place, j in enumerate(group):
             r_p[j] = sums[:, place * chunk : (place + 1) * chunk]
         for j in group:
-            rcopy(r_p.at[j], r_pr.at[j], p_s.at[0], p_r.at[j], partner).start()
-
-    def send_across(at, j):
-        rcopy(r_y.at[at, j], r_yr.at[at, j], y_s.at[at], y_r.at[at, j], across).start()
+            rcopy(r_p.at[j], r_pr.at[j], p_s.at[0], p_r.at[j // 2], partner).start()
+
+    def send_across(at, j, send=0):
+        rcopy(r_y.at[at, j], r_yr.at[at, j], y_s.at[send], y_r.at[at, j // 2], across).start()
 
     far = jnp.where(2 * a >= na, 0, na - 1)
     cross_rows = block((1 - b) * na + a)
 
     def own_part(group):
         up_acc[:, : chunk * len(group)] = product(c, group)
-        for j in group:
-            rcopy(r_p.at[j], r_pr.at[j], p_s.at[0], p_r.at[j], partner).wait_recv()
+        for j in group[::2]:
+            view = r_pr.at[paired(j)]
+            rcopy(view, view, p_s.at[0], p_r.at[j // 2], partner).wait_recv()
         for place, j in enumerate(group):
             cols = slice(place * chunk, (place + 1) * chunk)
             other = (up_acc[y_other, cols] + r_pr[j, y_other].astype(F32)).astype(BF16)
@@ -524,7 +511,7 @@
 
             def beside(at, up_line, down_line):
                 way, to = (1, above) if up_line else (0, below)
-                rcopy(r_y.at[at, j], r_cr.at[way, j], c_s.at[way], c_r.at[way, j], to).start()
+                rcopy(r_y.at[at, j], r_cr.at[way, j], c_s.at[0], c_r.at[way], to).start()
 
             if j < r_turned:
                 at_distance(1, beside)
@@ -540,15 +527,18 @@
 
             @pl.when(inside)
             def _():
-                view = r_cr.at[way, j]
-                rcopy(view, view, c_s.at[0], c_r.at[way, j], across).wait_recv()
+                if j == 0:
+                    view = r_cr.at[way, pl.ds(0, r_turned)]
+                    rcopy(view, view, c_s.at[0], c_r.at[way], across).wait_recv()
                 cross[j] = cross[j] + r_cr[way, j].astype(F32)
 
         r_y[a, j] = cross[j].astype(BF16)
         send_across(a, j)
 
     def y_arrived(at, j):
-        rcopy(r_y.at[at, j], r_yr.at[at, j], y_s.at[at], y_r.at[at, j], across).wait_recv()
+        if j % 2 == 0:
+            view = r_yr.at[at, paired(j)]
+            rcopy(view, view, y_s.at[0], y_r.at[at, j // 2], across).wait_recv()
 
     def z_place(step, place):
         if step == 1 or na > 4:
@@ -557,8 +547,9 @@
 
     def z_add(step, place, at, j):
         index = z_place(step, place)
-        view = r_zr.at[index, j]
-        rcopy(view, view, z_s.at[0], z_r.at[index, j], across).wait_recv()
+        if j % 2 == 0:
+            view = r_zr.at[index, paired(j)]
+            rcopy(view, view, z_s.at[0], z_r.at[index, j // 2], across).wait_recv()
         keep[at, j] = keep[at, j] + r_zr[index, j].astype(F32)
 
     def gate_even(up_line):
@@ -592,7 +583,7 @@
                 to = dev(a + hop if up_line else a - hop, b, c)
                 index = z_place(hop, place)
                 rcopy(
-                    r_z.at[at, j], r_zr.at[index, j], z_s.at[0], z_r.at[index, j], to
+                    r_z.at[at, j], r_zr.at[index, j], z_s.at[0], z_r.at[index, j // 2], to
                 ).start()
 
             if d == 1:
@@ -619,7 +610,7 @@
         total = keep[a, j]
         res[0, j] = total[:rows]
         res[1, j] = total[rows:]
-        rcopy(res.at[oc, j], res_r.at[j], l_s.at[0], l_r.at[j], partner).start()
+        rcopy(res.at[oc, j], res_r.at[j], l_s.at[0], l_r.at[j // 2], partner).start()
 
     groups = [tuple(range(j, min(j + GROUPED, chunks))) for j in range(0, chunks, GROUPED)]
     send_partner(groups[0])
@@ -641,7 +632,7 @@
         at_distance(d, send_rest)
     shared_active()
     for j in range(r_turned, chunks):
-        at_distance(1, lambda at, up_line, down_line: send_across(at, j))
+        at_distance(1, lambda at, up_line, down_line: send_across(at, j, 1))
     for j in range(chunks):
         join(j)
     for d in range(na - 1, 2, -1):
@@ -661,7 +652,9 @@
         collect(j)
     shared_collect()
     for j in range(chunks):
-        rcopy(res.at[oc, j], res_r.at[j], l_s.at[0], l_r.at[j], partner).wait_recv()
+        if j % 2 == 0:
+            view = res_r.at[paired(j)]
+            rcopy(view, view, l_s.at[0], l_r.at[j // 2], partner).wait_recv()
         own_cols = pl.ds(pl.multiple_of(c * half + j * chunk, LANES), chunk)
         other_cols = pl.ds(pl.multiple_of(oc * half + j * chunk, LANES), chunk)
         acc[:, own_cols] = res[c, j]
@@ -683,26 +676,33 @@
     def _():
         rcopy(x_win, x_win, win_s.at[0], win_r.at[0], partner).wait_send()
 
-    for d in range(na):
-        x_sent(d)
+    for at in range(na):
+
+        @pl.when(a == at)
+        def _():
+            left = x_sent(at)
+            while left:
+                some = min(left, nc)
+                view = x_all.at[c, pl.ds(0, some * pair)]
+                rcopy(view, view, xy_s.at[0], x_r.at[0, 0], partner).wait_send()
+                left -= some
+
     view = x_all.at[c]
     rcopy(view, view, xp_s.at[0], xp_r.at[0], partner).wait_send()
     rcopy(r_p, r_pr, p_s.at[0], p_r.at[0], partner).wait_send()
-    for d in range(na):
-        first = r_turned if d == 1 else 0
-
-        def y_sent(at, up_line, down_line):
-            view = r_y.at[at, pl.ds(first, chunks - first)]
-            rcopy(view, view, y_s.at[at], y_r.at[0, 0], across).wait_send()
-
-        if first < chunks:
-            at_distance(d, y_sent)
-    for way, inside in ((0, a > 0), (1, a < na - 1)) if r_turned else ():
-
-        @pl.when(inside)
+    for at in range(na):
+        beside = (at > 0) + (at < na - 1)
+
+        @pl.when(a == at)
         def _():
-            view = r_cr.at[way, pl.ds(0, r_turned)]
-            rcopy(view, view, c_s.at[way], c_r.at[0, 0], across).wait_send()
+            if r_turned:
+                view = r_y.at[pl.ds(0, beside), pl.ds(0, r_turned)]
+                rcopy(view, view, c_s.at[0], c_r.at[0], across).wait_send()
+            view = r_y.at[pl.ds(0, na - beside)]
+            rcopy(view, view, y_s.at[0], y_r.at[0, 0], across).wait_send()
+            if r_turned < chunks:
+                view = r_y.at[pl.ds(0, beside), pl.ds(0, chunks - r_turned)]
+                rcopy(view, view, y_s.at[1], y_r.at[0, 0], across).wait_send()
 
     view = r_z.at[pl.ds(0, na - 1)]
     rcopy(view, view, z_s.at[0], z_r.at[0, 0], across).wait_send()
@@ -747,6 +747,7 @@
     x_count = half // x_chunk
     x_turned = min(X_TURNED, x_count)
     r_turned = min(R_TURNED, chunks)
+    pairs = (chunks + 1) // 2
     z_places = 2 * na + 2 if na > 4 else na + 3
     return pl.pallas_call(
         functools.partial(layer_kernel, n, EXPERTS, group, chunk, window, x_chunk, x_turned, r_turned),
@@ -788,9 +789,7 @@
             dma((2,)),
             dma((1,)),
             dma((1,)),
-            dma((2, 2, na)),
-            dma((2,)),
-            dma((na,)),
+            dma((1,)),
             dma((1,)),
             dma((nc, x_count)),
             dma((x_count,)),
@@ -799,15 +798,15 @@
             dma((2,)),
             dma((2,)),
             dma((1,)),
-            dma((chunks,)),
+            dma((pairs,)),
+            dma((1,)),
             dma((2,)),
-            dma((2, chunks)),
-            dma((na,)),
-            dma((na, chunks)),
+            dma((2,)),
+            dma((na, pairs)),
             dma((1,)),
-            dma((z_places, chunks)),
+            dma((z_places, pairs)),
             dma((1,)),
-            dma((chunks,)),
+            dma((pairs,)),
         ],
         compiler_params=pltpu.CompilerParams(
             collective_id=0, has_side_effects=True, vmem_limit_bytes=67_043_328

time: 49.9 us -> 48.2 us (0.966)
  Pallas kernels: 48.1 us -> 46.5 us
    pallas_call x1, Pallas kernels: 48.1 us -> 46.5 us  [per_device(): pl.pallas_call(functools.partial(layer_kernel, n, EXPERTS, group, chunk,...]
where the time goes in v4:
time: 48.2 us; the launch traced here: 48.1 us
  Pallas kernels  46.5 us (96%)
  local copies, waits for them, and re-layouts  1.59 us (3%)
    pallas_call x1, Pallas kernels, per_device(): pl.pallas_call(functools.partial(layer_kernel, n, EXPERTS, group, chunk,...  46.5 us
    unnamed x1, local copies, waits for them, and re-layouts  1.59 us

profile of v4, /device:TPU:0, one launch (start us, length us, event | category | flops | bytes accessed | tf_op | source)
XLA Modules:
  0.0 48.1 jit_solution(15521423282563071378)
XLA Ops:
  0.0 46.5 %shard_map.91 = bf16[2,4,7168]{2,1,0:T(4,128)(2,1)} custom-call(bf16[2,4,7168]{2,1,0:T(4,128)(2,1)} %tokens_ref.1, s32[1,2]{1,0:T(1,128)} %bitcast.3, s32[1,2,4,8]{3,2,1,0:T(4,128)} %ids_ref.1, f32[1,2,4,8]{3,2,1,0:T(4,128)} %gates_ref.1, f32[1,7168]{1,0:T(1,128)} %gain_ref.1, bf16[1,1,7168,2048]{3,2,1,0:T(8,128)(2,1)} %gate_up_hbm.1, ...), custom_call_target="tpu_custom_call" | custom-call | tf_op jit(solution)/shard_map/pallas_call | solution.py:752
  46.5 1.6 %copy.11 = bf16[2,4,7168]{2,1,0:T(4,128)(2,1)} copy(bf16[2,4,7168]{2,1,0:T(4,128)(2,1)} %shard_map.91) | data formatting | bytes 229376

commit v5 on v4

--- a/solution.py
+++ b/solution.py
@@ -617,6 +617,8 @@
     for at, group in enumerate(groups):
         if at + 1 < len(groups):
             send_partner(groups[at + 1])
+        if at == len(groups) - 1:
+            shared_active()
         own_part(group)
         for j in group:
             if j < r_turned:
@@ -630,7 +632,6 @@
                     send_across(at, j)
 
         at_distance(d, send_rest)
-    shared_active()
     for j in range(r_turned, chunks):
         at_distance(1, lambda at, up_line, down_line: send_across(at, j, 1))
     for j in range(chunks):

time: 48.2 us -> 47.6 us (0.988)
  Pallas kernels: 46.5 us -> 45.8 us
    pallas_call x1, Pallas kernels: 46.5 us -> 45.8 us  [per_device(): pl.pallas_call(functools.partial(layer_kernel, n, EXPERTS, group, chunk,...]
where the time goes in v5:
time: 47.6 us; the launch traced here: 47.4 us
  Pallas kernels  45.8 us (96%)
  local copies, waits for them, and re-layouts  1.59 us (3%)
    pallas_call x1, Pallas kernels, per_device(): pl.pallas_call(functools.partial(layer_kernel, n, EXPERTS, group, chunk,...  45.8 us
    unnamed x1, local copies, waits for them, and re-layouts  1.59 us

profile of v5, /device:TPU:0, one launch (start us, length us, event | category | flops | bytes accessed | tf_op | source)
XLA Modules:
  0.0 47.4 jit_solution(6162986636382686925)
XLA Ops:
  0.0 45.8 %shard_map.91 = bf16[2,4,7168]{2,1,0:T(4,128)(2,1)} custom-call(bf16[2,4,7168]{2,1,0:T(4,128)(2,1)} %tokens_ref.1, s32[1,2]{1,0:T(1,128)} %bitcast.3, s32[1,2,4,8]{3,2,1,0:T(4,128)} %ids_ref.1, f32[1,2,4,8]{3,2,1,0:T(4,128)} %gates_ref.1, f32[1,7168]{1,0:T(1,128)} %gain_ref.1, bf16[1,1,7168,2048]{3,2,1,0:T(8,128)(2,1)} %gate_up_hbm.1, ...), custom_call_target="tpu_custom_call" | custom-call | tf_op jit(solution)/shard_map/pallas_call | solution.py:753
  45.8 1.6 %copy.11 = bf16[2,4,7168]{2,1,0:T(4,128)(2,1)} copy(bf16[2,4,7168]{2,1,0:T(4,128)(2,1)} %shard_map.91) | data formatting | bytes 229376
